TPU v7x, 256 devices: a whole 4x4x8 slice. The times are simulated.
256 devices in a mesh: lon: 16 (over z, x_hi), lat: 4 (over y), mem: 4 (over x_lo, core).
Axes of the slice: x: 4 (x_hi: 2, x_lo: 2; x = x_hi * 2 + x_lo), y: 4, z: 8, core: 2. Of those that a mesh axis runs over, the one named last changes fastest.
Arguments:
- anomalies: bfloat16 [32, 4, 1024, 512], P('mem', None, 'lon', 'lat'), may hold values from -6 to 6
- spread: float32 [4, 1024, 512], P(None, 'lon', 'lat'), may hold values from 0.5 to 2
- obs_index: int32 [16, 4, 2048], P('lon', 'lat'), may hold values from 0 to 32767
- innovation: float32 [16, 4, 2048], P('lon', 'lat'), may hold values from -6 to 6
- obs_weight: float32 [16, 4, 2048], P('lon', 'lat'), may hold values from 0.5 to 8
- band_width: int32 [2, 4], replicated, may hold values from 6 to 12, as said below
Outputs:
- control_ens: float32 [32, 4, 1024, 512], P('mem', None, 'lon', 'lat')
- control_static: float32 [4, 1024, 512], P(None, 'lon', 'lat')
Inputs may be any that keep to these rules, and one draw needn't show every extreme that they name: `obs_index`: A cell of the tile's 4 x 64 x 128 block, flattened with latitude fastest. `band_width`: in each of the two rows some level has exactly 12.
All inputs are finite; a program needn't handle non-finite values.
Results may differ from a plain program's by a relative error of at most 0.0003.
Values may be sent and summed in bfloat16 or wider, within the bound.
A program may use at most 64 MiB of HBM per device.

v0:
```python
import math

import jax
import jax.numpy as jnp
from jax import lax
from jax.experimental import pallas as pl
from jax.experimental.pallas import tpu as pltpu
from jax.sharding import PartitionSpec as P

BAND = 12
HALO = 2 * BAND
PAD = 32
hybrid_ens = 0.75
hybrid_static = 0.25
F32, BF16 = jnp.float32, jnp.bfloat16
HI = lax.Precision.HIGHEST
MESH = pl.DeviceIdType.MESH
AROUND = [(dx, dy) for dy in (0, 1, -1) for dx in (1, -1, 0) if (dx, dy) != (0, 0)]


def iota(shape, axis):
    return lax.broadcasted_iota(jnp.int32, shape, axis)


def dot(a, b, precision=None):
    return jnp.dot(a, b, preferred_element_type=F32, precision=precision)


def split(x):
    high = x.astype(BF16)
    return high, (x - high.astype(F32)).astype(BF16)


def kernel(dims, band_ref, a_ref, s_ref, idx_ref, inn_ref, wt_ref, p_ref, ps_ref, lam_ref,
           ac, kl, kr, hl, hr, f0c, k0l, k0r, f0l, f0r, f1c, k1l, k1r, f1l, f1r,
           obs, mlat, nlon, xs, ub, sb, y_ref, yr, t1_ref, gather_mem, gather_lat, gather_lon,
           a_send, a_recv, f0_send, f0_recv, f1_send, f1_recv, r0_send, r0_recv, r1_send, r1_recv,
           g_send, g_recv, q_send, q_recv, sm_send, sm_recv, sa_send, sa_recv, so_send, so_recv):
    n_lon, n_lat, n_mem, members, levels, rows, cols = dims
    lon, lat, mem = lax.axis_index("lon"), lax.axis_index("lat"), lax.axis_index("mem")
    ce2 = hybrid_ens / (members * n_mem)
    cs2 = hybrid_static
    ext = rows + 2 * PAD

    def at(dlon=0, dlat=0, dmem=0):
        return {
            "lon": lax.rem(lon + (dlon + n_lon), n_lon),
            "lat": lax.rem(lat + (dlat + n_lat), n_lat),
            "mem": lax.rem(mem + (dmem + n_mem), n_mem),
        }

    def copy(src, dst, send, recv, device):
        return pltpu.make_async_remote_copy(
            src_ref=src, dst_ref=dst, send_sem=send, recv_sem=recv, device_id=device, device_id_type=MESH
        )

    partners = [(dx, dy, 0) for dx, dy in AROUND]
    partners += [(0, 0, o) for o in range(1, n_mem)]
    partners += [(0, o, 0) for o in range(2, n_lat - 1)]
    partners += [(o, 0, 0) for o in range(2, n_lon - 1)]
    barrier = pltpu.get_barrier_semaphore()
    for partner in partners:
        pl.semaphore_signal(barrier, inc=1, device_id=at(*partner), device_id_type=MESH)

    own = pl.ds(PAD, rows)
    low, high = pl.ds(PAD - HALO, HALO), pl.ds(PAD + rows, HALO)
    first, last = pl.ds(0, HALO), pl.ds(rows - HALO, HALO)

    sel_row, sel_col = iota((levels * cols, 2 * cols), 0), iota((levels * cols, 2 * cols), 1)
    sel_level, sel_lat = sel_row // cols, lax.rem(sel_row, cols)
    spot = lax.rem(sel_col, cols) - HALO * sel_level
    wanted = jnp.where(sel_col < cols, spot + (cols - HALO), spot)
    select = jnp.where((spot >= 0) & (spot < HALO) & (sel_lat == wanted), 1.0, 0.0)

    packed = dot(
        jnp.concatenate([a_ref[:, l].reshape(members * rows, cols) for l in range(levels)], axis=1),
        select.astype(BF16),
    ).astype(BF16)
    kl[...] = packed[:, :cols].reshape(members, rows, cols)
    kr[...] = packed[:, cols:].reshape(members, rows, cols)
    edges = (pl.ds(0, PAD - HALO), pl.ds(PAD + rows + HALO, PAD - HALO))
    for edge in edges:
        ac[:, :, edge, :] = jnp.zeros((members, levels, PAD - HALO, cols), BF16)
        for ref in (hl, hr):
            ref[:, edge, :] = jnp.zeros((members, PAD - HALO, cols), BF16)
        for ref in (f0c, f0l, f0r, f1c, f1l, f1r):
            ref[:, edge, :] = jnp.zeros((ref.shape[0], PAD - HALO, cols), F32)
    ac[:, :, own, :] = a_ref[...]
    f0c[levels, own, :] = s_ref[mem]

    r, c = iota((cols, cols), 0), iota((cols, cols), 1)
    inside_low = jnp.where(lat > 0, 1.0, 0.0).astype(F32)
    inside_high = jnp.where(lat < n_lat - 1, 1.0, 0.0).astype(F32)
    offsets = iota((8, cols), 1) - BAND

    def level_matrices(l, carry):
        def band_of(which):
            width = jnp.full((1, 1), band_ref[which, l].astype(F32), F32)

            def raw(diff):
                d = diff.astype(F32)
                ratio = d / (0.5 * width)
                return jnp.where(jnp.abs(d) <= width, jnp.exp(-0.5 * (ratio * ratio)), 0.0)

            total = jnp.sum(raw(offsets), axis=1, keepdims=True)[0:1]
            return lambda diff: raw(diff) / total

        band = band_of(1)
        spot = r - HALO * l
        valid = jnp.where((spot >= 0) & (spot < HALO), 1.0, 0.0)
        d0, dm, dp = band(r - c), band(r - cols - c), band(r + cols - c)
        from_low = spot + (cols - HALO)
        dml, d0l = band(from_low - cols - c) * valid, band(from_low - c) * valid
        dpr, d0r = band(spot + cols - c) * valid, band(spot - c) * valid
        twice = [
            dot(d0, d0, HI) + inside_low * dot(dp, dm, HI) + inside_high * dot(dm, dp, HI),
            inside_low * (dot(d0l, dm, HI) + dot(dml, d0, HI)),
            inside_high * (dot(d0r, dp, HI) + dot(dpr, d0, HI)),
        ]
        once = [d0, inside_low * dml, inside_high * dpr]
        for part in range(3):
            hi, lo = split(jnp.concatenate([twice[part], once[part]], axis=1))
            mlat[l, part * cols:(part + 1) * cols, :] = hi
            mlat[l, (3 + part) * cols:(4 + part) * cols, :] = hi
            mlat[l, (6 + part) * cols:(7 + part) * cols, :] = lo
        band = band_of(0)
        near = band(iota((rows, ext), 0) + PAD - iota((rows, ext), 1))
        far = band(iota((ext, ext), 0) - iota((ext, ext), 1))
        for which, matrix in enumerate((dot(near, far, HI), near)):
            hi, lo = split(matrix)
            nlon[which, l, 0:rows, :] = hi
            nlon[which, l, rows:2 * rows, :] = lo
        return carry

    lax.fori_loop(0, levels, level_matrices, 0)

    pl.semaphore_wait(barrier, len(partners))

    def halo(centre, source, left, right, packed_left, packed_right, send, recv):
        copies = []
        for number, (dx, dy) in enumerate(AROUND):
            from_rows = {1: last, -1: first, 0: pl.ds(0, rows)}[dx]
            to_rows = {1: low, -1: high, 0: own}[dx]
            if dy == 0:
                src, dst = source(dx), centre.at[..., to_rows, :] if len(centre.shape) == 3 else centre.at[:, :, to_rows, :]
            else:
                src = (packed_left if dy == 1 else packed_right).at[:, from_rows, :]
                dst = (left if dy == 1 else right).at[:, to_rows, :]
            one = copy(src, dst, send.at[number], recv.at[number], at(dx, dy))
            one.start()
            copies.append(one)
        return copies

    a_copies = halo(ac, lambda dx: a_ref.at[:, :, last if dx == 1 else first, :], hl, hr, kl, kr, a_send, a_recv)

    index = idx_ref[...]
    weight = wt_ref[...]
    at_row, at_col = index // cols, lax.rem(index, cols)
    count = index.shape[1]
    columns = jnp.where(iota((cols, count), 0) == at_col, 1.0, 0.0).astype(BF16)

    def thirds(v):
        one = v.astype(BF16).astype(F32)
        two = (v - one).astype(BF16).astype(F32)
        return [one, two, v - one - two]

    terms = thirds(weight) + thirds(weight * inn_ref[...])

    def level_fields(l, carry):
        here = (iota((rows, count), 0) + rows * l) == at_row
        stacked = jnp.concatenate([jnp.where(here, t, 0.0).astype(BF16) for t in terms], axis=0)
        sums = lax.dot_general(stacked, columns, (((1,), (1,)), ((), ())), preferred_element_type=F32)
        obs[l] = sums[0:rows] + sums[rows:2 * rows] + sums[2 * rows:3 * rows]
        f0c[l, own, :] = sums[3 * rows:4 * rows] + sums[4 * rows:5 * rows] + sums[5 * rows:]
        return carry

    lax.fori_loop(0, levels, level_fields, 0)

    def pack(centre, left, right, slot):
        both = dot(jnp.concatenate([centre[l, own, :] for l in range(levels)], axis=1), select, HI)
        left[slot] = both[:, :cols]
        right[slot] = both[:, cols:]

    pack(f0c, k0l, k0r, 0)
    spot = lax.rem(iota((cols, 2 * cols), 1), cols) - HALO * mem
    wanted = jnp.where(iota((cols, 2 * cols), 1) < cols, spot + (cols - HALO), spot)
    mine = jnp.where((spot >= 0) & (spot < HALO) & (iota((cols, 2 * cols), 0) == wanted), 1.0, 0.0)
    both = dot(s_ref[mem], mine, HI)
    k0l[1] = both[:, :cols]
    k0r[1] = both[:, cols:]
    field_rows = {1: pl.ds(PAD + rows - HALO, HALO), -1: pl.ds(PAD, HALO)}
    f0_copies = halo(f0c, lambda dx: f0c.at[:, field_rows[dx], :], f0l, f0r, k0l, k0r, f0_send, f0_recv)
    for one in a_copies + f0_copies:
        one.wait_recv()

    def lon_pass(l, u_hi, u_lo, which):
        tall = dot(nlon[which, l], u_hi)
        return tall[0:rows] + tall[rows:] + dot(nlon[which, l, 0:rows, :], u_lo)

    def apply(centre, left, right, turn):
        zl, zr = left[0], right[0]
        for k in range(members):
            spans = pl.ds(k * ext, ext)
            for part, (rim, z) in enumerate(((hl, zl), (hr, zr))):
                hi, lo = split(rim[k].astype(F32) * z)
                xs[spans, (1 + part) * cols:(2 + part) * cols] = hi
                xs[spans, (4 + part) * cols:(5 + part) * cols] = lo

        def one_level(l, carry):
            z = centre[l]
            for k in range(members):
                hi, lo = split(ac[k, l].astype(F32) * z)
                xs[pl.ds(k * ext, ext), 0:cols] = hi
                xs[pl.ds(k * ext, ext), 3 * cols:4 * cols] = lo
            ub[...] = dot(xs[...], mlat[l, 0:6 * cols, :]) + dot(xs[:, 0:3 * cols], mlat[l, 6 * cols:, :])
            total = jnp.zeros((rows, cols), F32)
            for k in range(members):
                hi, lo = split(ub[pl.ds(k * ext, ext), :])
                total += a_ref[k, l].astype(F32) * lon_pass(l, hi[:, :cols], lo[:, :cols], 0)
                p_ref[turn, k, l] = math.sqrt(ce2) * lon_pass(l, hi[:, cols:], lo[:, cols:], 1)
            y_ref[l] = ce2 * total
            return carry

        lax.fori_loop(0, levels, one_level, 0)
        his, los = [], []
        for stat, z in ((f0c[levels], centre[mem]), (f0l[1], zl), (f0r[1], zr)):
            hi, lo = split(stat * z)
            his.append(hi)
            los.append(lo)
        u = dot(jnp.concatenate(his + los, axis=1), mlat[mem, 0:6 * cols, :])
        u += dot(jnp.concatenate(his, axis=1), mlat[mem, 6 * cols:, :])
        hi, lo = split(u)
        y_ref[mem] = y_ref[mem] + cs2 * s_ref[mem] * lon_pass(mem, hi[:, :cols], lo[:, :cols], 0)
        ps_ref[turn, mem] = math.sqrt(cs2) * lon_pass(mem, hi[:, cols:], lo[:, cols:], 1)

    def reduced(slots, send, recv):
        copies = []
        for o in range(1, n_mem):
            peer = lax.rem(mem + o, n_mem)
            one = copy(y_ref.at[peer], slots.at[o - 1], send.at[o - 1], recv.at[o - 1], at(0, 0, o))
            one.start()
            copies.append(one)
        for one in copies:
            one.wait()
        return y_ref[mem] + slots[0] + slots[1] + slots[2]

    apply(f0c, f0l, f0r, 0)
    y0 = reduced(yr.at[0], r0_send, r0_recv)
    t0 = f0c[mem, own, :]
    t1 = obs[mem] * y0
    t1_ref[...] = t1
    f1c[mem, own, :] = t1
    g_copies = []
    for o in range(1, n_mem):
        one = copy(t1_ref, f1c.at[mem, own, :], g_send.at[o - 1], g_recv.at[o - 1], at(0, 0, o))
        one.start()
        g_copies.append(one)
    for one in g_copies:
        one.wait_recv()
    pack(f1c, k1l, k1r, 0)
    f1_copies = halo(f1c, lambda dx: f1c.at[:, field_rows[dx], :], f1l, f1r, k1l, k1r, f1_send, f1_recv)
    for one in f1_copies:
        one.wait_recv()
    apply(f1c, f1l, f1r, 1)
    y1 = reduced(yr.at[1], r1_send, r1_recv)

    q_copies = []
    for turn in range(2):
        sb[turn] = ps_ref[turn, mem]
    for o in range(1, n_mem):
        one = copy(sb, ps_ref.at[:, mem], q_send.at[o - 1], q_recv.at[o - 1], at(0, 0, o))
        one.start()
        q_copies.append(one)

    def summed(x):
        return jnp.sum(jnp.sum(x, axis=0, keepdims=True), axis=1, keepdims=True)

    lane = iota((8, cols), 1)
    sums = jnp.zeros((8, cols), F32)
    for number, value in enumerate((t0 * y0, t1 * y0, t1 * y1, y1 * (obs[mem] * y1))):
        sums = jnp.where(lane == number, summed(value), sums)

    tail = []

    def total_over(value, slots, me, count, send, recv, step):
        slots[me] = value
        copies = []
        for o in range(1, count):
            one = copy(slots.at[me], slots.at[me], send.at[o - 1], recv.at[o - 1], at(*(o * s for s in step)))
            one.start()
            copies.append(one)
        for one in copies:
            one.wait_recv()
        tail.extend(copies)
        out = slots[0]
        for other in range(1, count):
            out = out + slots[other]
        return out

    sums = total_over(sums, gather_mem, mem, n_mem, sm_send, sm_recv, (0, 0, 1))
    sums = total_over(sums, gather_lat, lat, n_lat, sa_send, sa_recv, (0, 1, 0))
    sums = total_over(sums, gather_lon, lon, n_lon, so_send, so_recv, (1, 0, 0))
    row = sums[0:1]

    def pick(number):
        return jnp.sum(jnp.where(iota((1, cols), 1) == number, row, 0.0), axis=1, keepdims=True)

    rr = pick(0)
    u, v, s = pick(1) / rr, pick(2) / rr, pick(3) / rr
    alpha = 1.0 / (1.0 + u)
    beta = (v - u * u) * alpha * alpha
    g, h = 1.0 - alpha + beta, -alpha
    alpha_next = beta / (g * g * (1.0 + u) + 2.0 * g * h * (u + v) + h * h * (v + s))
    lam_ref[...] = jnp.where(lane == 0, alpha + alpha_next * g, alpha_next * h)

    for one in q_copies:
        one.wait()
    for one in a_copies + f0_copies + g_copies + f1_copies + tail:
        one.wait_send()


def per_device(n_lon, n_lat, n_mem, anomalies, spread, obs_index, innovation, obs_weight, band_width):
    members, levels, rows, cols = anomalies.shape
    ext = rows + 2 * PAD
    count = obs_index.shape[-1]
    vmem, dma = pltpu.VMEM, pltpu.SemaphoreType.DMA
    dims = (n_lon, n_lat, n_mem, members, levels, rows, cols)
    whole = pl.BlockSpec(memory_space=pltpu.VMEM)
    parts, static, lam = pl.pallas_call(
        lambda *refs: kernel(dims, *refs),
        out_shape=(
            jax.ShapeDtypeStruct((2, members, levels, rows, cols), F32),
            jax.ShapeDtypeStruct((2, levels, rows, cols), F32),
            jax.ShapeDtypeStruct((8, cols), F32),
        ),
        in_specs=[pl.BlockSpec(memory_space=pltpu.SMEM)] + [whole] * 5,
        out_specs=(whole, whole, whole),
        scratch_shapes=[
            vmem((members, levels, ext, cols), BF16),
            vmem((members, rows, cols), BF16), vmem((members, rows, cols), BF16),
            vmem((members, ext, cols), BF16), vmem((members, ext, cols), BF16),
            vmem((levels + 1, ext, cols), F32),
            vmem((2, rows, cols), F32), vmem((2, rows, cols), F32),
            vmem((2, ext, cols), F32), vmem((2, ext, cols), F32),
            vmem((levels, ext, cols), F32),
            vmem((1, rows, cols), F32), vmem((1, rows, cols), F32),
            vmem((1, ext, cols), F32), vmem((1, ext, cols), F32),
            vmem((levels, rows, cols), F32),
            vmem((levels, 9 * cols, 2 * cols), BF16),
            vmem((2, levels, 2 * rows, ext), BF16),
            vmem((members * ext, 6 * cols), BF16),
            vmem((members * ext, 2 * cols), F32),
            vmem((2, rows, cols), F32),
            vmem((levels, rows, cols), F32),
            vmem((2, n_mem - 1, rows, cols), F32),
            vmem((rows, cols), F32),
            vmem((n_mem, 8, cols), F32), vmem((n_lat, 8, cols), F32), vmem((n_lon, 8, cols), F32),
        ]
        + [dma((8,))] * 6
        + [dma((n_mem - 1,))] * 8
        + [dma((n_mem - 1,))] * 2
        + [dma((n_lat - 1,))] * 2
        + [dma((n_lon - 1,))] * 2,
        compiler_params=pltpu.CompilerParams(
            collective_id=0, has_side_effects=True, vmem_limit_bytes=48 * 1024 * 1024
        ),
    )(
        band_width, anomalies, spread, obs_index.reshape(1, count), innovation.reshape(1, count),
        obs_weight.reshape(1, count),
    )
    near, far = lam[0, 0], lam[0, 1]
    return near * parts[0] + far * parts[1], near * static[0] + far * static[1]


def solution(mesh):
    n_lon, n_lat, n_mem = (mesh.shape[name] for name in ("lon", "lat", "mem"))
    return jax.shard_map(
        lambda *args: per_device(n_lon, n_lat, n_mem, *args),
        mesh=mesh,
        in_specs=(
            P("mem", None, "lon", "lat"),
            P(None, "lon", "lat"),
            P("lon", "lat", None),
            P("lon", "lat", None),
            P("lon", "lat", None),
            P(),
        ),
        out_specs=(P("mem", None, "lon", "lat"), P(None, "lon", "lat")),
        check_vma=False,
    )
```

profile of v0, /device:TPU:1, one launch (start us, length us, event | category | flops | bytes accessed | tf_op | source)
XLA Modules:
  0.0 86.7 jit_solution(2785972160688654994)
XLA Ops:
  0.6 0.0 copy-start
  0.6 1.0 %copy-done = bf16[8,4,64,128]{3,2,1,0:T(8,128)(2,1)S(1)} copy-done((bf16[8,4,64,128]{3,2,1,0:T(8,128)(2,1)S(1)}, bf16[8,4,64,128]{3,2,1,0:T(8,128)(2,1)}, u32[]{:S(2)}) %copy-start) | copy-done | bytes 524312
  1.7 0.0 copy-start.1
  1.7 0.9 %copy-done.1 = f32[4,64,128]{2,1,0:T(8,128)S(1)} copy-done((f32[4,64,128]{2,1,0:T(8,128)S(1)}, f32[4,64,128]{2,1,0:T(8,128)}, u32[]{:S(2)}) %copy-start.1) | copy-done | bytes 131096
  2.6 0.0 copy-start.2
  2.6 0.7 copy-done.2
  3.3 0.0 copy-start.3
  3.3 0.7 copy-done.3
  4.0 0.0 copy-start.4
  4.0 0.7 copy-done.4
  4.7 0.0 copy-start.5
  4.7 0.7 copy-done.5
  5.4 76.3 %shard_map.77 = (f32[2,8,4,64,128]{4,3,2,1,0:T(8,128)S(1)}, f32[2,4,64,128]{3,2,1,0:T(8,128)S(1)}, f32[8,128]{1,0:T(8,128)S(1)}) custom-call(s32[2,4]{1,0:T(2,128)S(1)} %copy-done.5, bf16[8,4,64,128]{3,2,1,0:T(8,128)(2,1)S(1)} %copy-done, f32[4,64,128]{2,1,0:T(8,128)S(1)} %copy-done.1, s32[1,2048]{1,0:T(1,128)S(1)} %bitcast.9, f32[1,2048]{1,0:T(1,128)S(1)} %bitcast.10, ...), custom_call_target="tpu_custom_call" | custom-call | tf_op jit(solution)/shard_map/pallas_call | solution.py:329
  81.7 0.7 fusion
  82.3 1.9 %add_bitcast_fusion.1 = f32[4,64,128]{2,1,0:T(8,128)} fusion(f32[2,4,64,128]{3,2,1,0:T(8,128)S(1)} %get-tuple-element.7, f32[]{:T(128)} %bitcast.4, f32[]{:T(128)} %bitcast.3), kind=kLoop, calls=%fused_computation.1 | loop fusion | flops 98304 | bytes 393224 | tf_op jit(solution)/shard_map/add | solution.py:372
  84.2 2.4 %add_bitcast_fusion = f32[8,4,64,128]{3,2,1,0:T(8,128)} fusion(f32[2,8,4,64,128]{4,3,2,1,0:T(8,128)S(1)} %get-tuple-element.6, f32[]{:T(128)} %bitcast.4, f32[]{:T(128)} %bitcast.3), kind=kLoop, calls=%fused_computation | loop fusion | flops 786432 | bytes 3145736 | tf_op jit(solution)/shard_map/add | solution.py:372
Async XLA Ops:
  0.6 1.0 %copy-start = (bf16[8,4,64,128]{3,2,1,0:T(8,128)(2,1)S(1)}, bf16[8,4,64,128]{3,2,1,0:T(8,128)(2,1)}, u32[]{:S(2)}) copy-start(bf16[8,4,64,128]{3,2,1,0:T(8,128)(2,1)} %refs_1_.1) | copy-start | bytes 1572868
  1.7 0.9 %copy-start.1 = (f32[4,64,128]{2,1,0:T(8,128)S(1)}, f32[4,64,128]{2,1,0:T(8,128)}, u32[]{:S(2)}) copy-start(f32[4,64,128]{2,1,0:T(8,128)} %refs_2_.1) | copy-start | bytes 393220
  2.6 0.7 copy-start.2
  3.3 0.7 copy-start.3
  4.0 0.7 copy-start.4
  4.7 0.7 copy-start.5
where the time goes:
time: 87 us; the launch traced here: 86.7 us
  Pallas kernels  76.3 us (88%)
  local copies, waits for them, and re-layouts  5.36 us (6%)
  other arithmetic  4.34 us (5%)
    pallas_call x1, Pallas kernels, per_device(): pl.pallas_call(lambda *refs: kernel(dims, *refs), out_shape=(jax.ShapeDty...  76.3 us
    unnamed x12, local copies, waits for them, and re-layouts  4.71 us
    add x1, other arithmetic, per_device(): near * parts[0] + far * parts[1]  2.43 us
    add x1, other arithmetic, per_device(): near * static[0] + far * static[1]  1.91 us

commit v1 on v0

v1 whole, which is shorter than its diff:
```python
import math

import jax
import jax.numpy as jnp
from jax import lax
from jax.experimental import pallas as pl
from jax.experimental.pallas import tpu as pltpu
from jax.sharding import PartitionSpec as P

BAND = 12
HALO = 2 * BAND
PAD = 32
CHUNKS = 4
hybrid_ens = 0.75
hybrid_static = 0.25
F32, BF16 = jnp.float32, jnp.bfloat16
HI = lax.Precision.HIGHEST
MESH = pl.DeviceIdType.MESH
AROUND = [(dx, dy) for dy in (0, 1, -1) for dx in (1, -1, 0) if (dx, dy) != (0, 0)]


def iota(shape, axis):
    return lax.broadcasted_iota(jnp.int32, shape, axis)


def dot(a, b, precision=None):
    return jnp.dot(a, b, preferred_element_type=F32, precision=precision)


def split(x):
    high = x.astype(BF16)
    return high, (x - high.astype(F32)).astype(BF16)


def kernel(dims, band_any, a_any, s_any, idx_any, inn_any, wt_any, ens_out, static_out,
           band_ref, idx_ref, inn_ref, wt_ref, ac, kl, kr, hl, hr, f0c, k0l, k0r, f0l, f0r, f1c, k1l, k1r, f1l, f1r,
           obs, mlat, nlon, xs, ub, us, p_ref, ps_ref, sl, y_ref, yr, t1_ref, gather_plane, gather_lon,
           in_sem, a_send, a_recv, f0_send, f0_recv, f1_send, f1_recv, r0_send, r0_recv, r1_send, r1_recv,
           g_send, g_recv, q0_send, q0_recv, q1_send, q1_recv, sp_send, sp_recv, so_send, so_recv, out_sem):
    n_lon, n_lat, n_mem, members, levels, rows, cols = dims
    lon, lat, mem = lax.axis_index("lon"), lax.axis_index("lat"), lax.axis_index("mem")
    ce2 = hybrid_ens / (members * n_mem)
    cs2 = hybrid_static
    ext = rows + 2 * PAD

    def at(dlon=0, dlat=0, dmem=0):
        return {
            "lon": lax.rem(lon + (dlon + n_lon), n_lon),
            "lat": lax.rem(lat + (dlat + n_lat), n_lat),
            "mem": lax.rem(mem + (dmem + n_mem), n_mem),
        }

    def copy(src, dst, send, recv, device):
        return pltpu.make_async_remote_copy(
            src_ref=src, dst_ref=dst, send_sem=send, recv_sem=recv, device_id=device, device_id_type=MESH
        )

    plane = [(0, ol, om) for ol in range(n_lat) for om in range(n_mem) if (ol, om) != (0, 0)]
    line = [(o, 0, 0) for o in range(1, n_lon)]
    partners = sorted({(dx % n_lon, dy % n_lat, 0) for dx, dy in AROUND} | set(plane) | set(line))
    barrier = pltpu.get_barrier_semaphore()
    for partner in partners:
        pl.semaphore_signal(barrier, inc=1, device_id=at(*partner), device_id_type=MESH)

    own = pl.ds(PAD, rows)
    inputs = [
        pltpu.make_async_copy(src, dst, in_sem.at[number])
        for number, (src, dst) in enumerate((
            (a_any, ac.at[:, :, own, :]), (s_any.at[mem], f0c.at[levels, own, :]), (band_any, band_ref),
            (idx_any, idx_ref), (inn_any, inn_ref), (wt_any, wt_ref),
        ))
    ]
    for one in inputs:
        one.start()
    low, high = pl.ds(PAD - HALO, HALO), pl.ds(PAD + rows, HALO)
    first, last = pl.ds(0, HALO), pl.ds(rows - HALO, HALO)

    sel_row, sel_col = iota((levels * cols, 2 * cols), 0), iota((levels * cols, 2 * cols), 1)
    sel_level, sel_lat = sel_row // cols, lax.rem(sel_row, cols)
    spot = lax.rem(sel_col, cols) - HALO * sel_level
    wanted = jnp.where(sel_col < cols, spot + (cols - HALO), spot)
    select = jnp.where((spot >= 0) & (spot < HALO) & (sel_lat == wanted), 1.0, 0.0)

    for one in inputs:
        one.wait()
    packed = dot(
        jnp.concatenate([ac[:, l, own, :].reshape(members * rows, cols) for l in range(levels)], axis=1),
        select.astype(BF16),
    ).astype(BF16)
    kl[...] = packed[:, :cols].reshape(members, rows, cols)
    kr[...] = packed[:, cols:].reshape(members, rows, cols)
    edges = (pl.ds(0, PAD - HALO), pl.ds(PAD + rows + HALO, PAD - HALO))
    for edge in edges:
        ac[:, :, edge, :] = jnp.zeros((members, levels, PAD - HALO, cols), BF16)
        for ref in (hl, hr):
            ref[:, edge, :] = jnp.zeros((members, PAD - HALO, cols), BF16)
        for ref in (f0c, f0l, f0r, f1c, f1l, f1r):
            ref[:, edge, :] = jnp.zeros((ref.shape[0], PAD - HALO, cols), F32)

    pl.semaphore_wait(barrier, len(partners))

    from_rows = {1: last, -1: first, 0: pl.ds(0, rows)}
    field_rows = {1: pl.ds(PAD + rows - HALO, HALO), -1: pl.ds(PAD, HALO)}
    to_rows = {1: low, -1: high, 0: own}

    def halo(centre, left, right, packed_left, packed_right, send, recv, chunk=None):
        copies = []
        for number, (dx, dy) in enumerate(AROUND):
            if dy == 0:
                if chunk is None:
                    src, dst = centre.at[:, field_rows[dx], :], centre.at[:, to_rows[dx], :]
                else:
                    src, dst = centre.at[chunk, :, field_rows[dx], :], centre.at[chunk, :, to_rows[dx], :]
            else:
                every = slice(None) if chunk is None else chunk
                src = (packed_left if dy == 1 else packed_right).at[every, from_rows[dx], :]
                dst = (left if dy == 1 else right).at[every, to_rows[dx], :]
            one = copy(src, dst, send.at[number], recv.at[number], at(dx, dy))
            one.start()
            copies.append(one)
        return copies

    batch = members // CHUNKS

    def send_chunk(number):
        return halo(ac, hl, hr, kl, kr, a_send.at[number], a_recv.at[number], pl.ds(number * batch, batch))

    a_copies = [send_chunk(0)]

    index = idx_ref[...]
    weight = wt_ref[...]
    at_row, at_col = index // cols, lax.rem(index, cols)
    count = index.shape[1]
    columns = jnp.where(iota((cols, count), 0) == at_col, 1.0, 0.0).astype(BF16)

    def thirds(v):
        one = v.astype(BF16).astype(F32)
        two = (v - one).astype(BF16).astype(F32)
        return [one, two, v - one - two]

    terms = thirds(weight) + thirds(weight * inn_ref[...])

    def level_fields(l, carry):
        here = (iota((rows, count), 0) + rows * l) == at_row
        stacked = jnp.concatenate([jnp.where(here, t, 0.0).astype(BF16) for t in terms], axis=0)
        sums = lax.dot_general(stacked, columns, (((1,), (1,)), ((), ())), preferred_element_type=F32)
        obs[l] = sums[0:rows] + sums[rows:2 * rows] + sums[2 * rows:3 * rows]
        f0c[l, own, :] = sums[3 * rows:4 * rows] + sums[4 * rows:5 * rows] + sums[5 * rows:]
        return carry

    lax.fori_loop(0, levels, level_fields, 0)

    def pack(centre, left, right, extra=0.0):
        both = dot(jnp.concatenate([centre[l, own, :] for l in range(levels)], axis=1), select, HI) + extra
        left[0] = both[:, :cols]
        right[0] = both[:, cols:]

    spare = levels * HALO
    spot = lax.rem(iota((cols, 2 * cols), 1), cols) - spare
    wanted = jnp.where(iota((cols, 2 * cols), 1) < cols, spot + (cols - HALO), spot)
    place = jnp.where((spot >= 0) & (spot < HALO) & (iota((cols, 2 * cols), 0) == wanted), 1.0, 0.0)
    pack(f0c, k0l, k0r, dot(f0c[levels, own, :], place, HI))
    f0_copies = halo(f0c, f0l, f0r, k0l, k0r, f0_send, f0_recv)
    a_copies.append(send_chunk(1))
    r, c = iota((cols, cols), 0), iota((cols, cols), 1)
    inside_low = jnp.where(lat > 0, 1.0, 0.0).astype(F32)
    inside_high = jnp.where(lat < n_lat - 1, 1.0, 0.0).astype(F32)
    offsets = iota((8, cols), 1) - BAND

    def level_matrices(l, carry):
        def band_of(which):
            width = jnp.full((1, 1), band_ref[which, l].astype(F32), F32)

            def raw(diff):
                d = diff.astype(F32)
                ratio = d / (0.5 * width)
                return jnp.where(jnp.abs(d) <= width, jnp.exp(-0.5 * (ratio * ratio)), 0.0)

            total = jnp.sum(raw(offsets), axis=1, keepdims=True)[0:1]
            return lambda diff: raw(diff) / total

        band = band_of(1)
        spot = r - HALO * l
        valid = jnp.where((spot >= 0) & (spot < HALO), 1.0, 0.0)
        d0, dm, dp = band(r - c), band(r - cols - c), band(r + cols - c)
        from_low = spot + (cols - HALO)
        dml, d0l = band(from_low - cols - c) * valid, band(from_low - c) * valid
        dpr, d0r = band(spot + cols - c) * valid, band(spot - c) * valid
        twice = [
            dot(d0, d0, HI) + inside_low * dot(dp, dm, HI) + inside_high * dot(dm, dp, HI),
            inside_low * (dot(d0l, dm, HI) + dot(dml, d0, HI)),
            inside_high * (dot(d0r, dp, HI) + dot(dpr, d0, HI)),
        ]
        once = [d0, inside_low * dml, inside_high * dpr]
        for part in range(3):
            hi, lo = split(jnp.concatenate([twice[part], once[part]], axis=1))
            mlat[l, part * cols:(part + 1) * cols, :] = hi
            mlat[l, (3 + part) * cols:(4 + part) * cols, :] = hi
            mlat[l, (6 + part) * cols:(7 + part) * cols, :] = lo
        band = band_of(0)
        near = band(iota((rows, ext), 0) + PAD - iota((rows, ext), 1))
        far = band(iota((ext, ext), 0) - iota((ext, ext), 1))
        for which, matrix in enumerate((dot(near, far, HI), near)):
            hi, lo = split(matrix)
            nlon[which, l, 0:rows, :] = hi
            nlon[which, l, rows:2 * rows, :] = lo
        return carry

    lax.fori_loop(0, levels, level_matrices, 0)

    for one in f0_copies:
        one.wait_recv()
    a_copies.append(send_chunk(2))
    realign = jnp.where((r - spare == c - HALO * mem) & (r >= spare) & (r < spare + HALO), 1.0, 0.0)
    sl[0] = dot(f0l[0], realign, HI)
    sl[1] = dot(f0r[0], realign, HI)

    def lon_pass(l, u_hi, u_lo, which):
        tall = dot(nlon[which, l], u_hi)
        return tall[0:rows] + tall[rows:] + dot(nlon[which, l, 0:rows, :], u_lo)

    def apply_members(centre, left, right, start, count):
        zl, zr = left[0], right[0]
        z = [centre[l] for l in range(levels)]
        chunk = pl.ds(start * ext, count * ext)
        for k in range(start, start + count):
            spans = pl.ds(k * ext, ext)
            for part, (rim, zz) in enumerate(((hl, zl), (hr, zr))):
                hi, lo = split(rim[k].astype(F32) * zz)
                for l in range(levels):
                    xs[l, spans, (1 + part) * cols:(2 + part) * cols] = hi
                    xs[l, spans, (4 + part) * cols:(5 + part) * cols] = lo
            for l in range(levels):
                hi, lo = split(ac[k, l].astype(F32) * z[l])
                xs[l, spans, 0:cols] = hi
                xs[l, spans, 3 * cols:4 * cols] = lo
        for l in range(levels):
            ub[l, chunk, :] = dot(xs[l, chunk, :], mlat[l, 0:6 * cols, :]) + dot(
                xs[l, chunk, 0:3 * cols], mlat[l, 6 * cols:, :]
            )
        for l in range(levels):
            total = jnp.zeros((rows, cols), F32)
            for k in range(start, start + count):
                hi, lo = split(ub[l, pl.ds(k * ext, ext), 0:cols])
                total += ac[k, l, own, :].astype(F32) * lon_pass(l, hi, lo, 0)
            y_ref[l] = ce2 * total if start == 0 else y_ref[l] + ce2 * total

    def apply_static(centre, left, right):
        his, los = [], []
        for stat, z in ((f0c[levels], centre[mem]), (sl[0], left[0]), (sl[1], right[0])):
            hi, lo = split(stat * z)
            his.append(hi)
            los.append(lo)
        u = dot(jnp.concatenate(his + los, axis=1), mlat[mem, 0:6 * cols, :])
        us[...] = u + dot(jnp.concatenate(his, axis=1), mlat[mem, 6 * cols:, :])
        hi, lo = split(us[:, 0:cols])
        y_ref[mem] = y_ref[mem] + cs2 * f0c[levels, own, :] * lon_pass(mem, hi, lo, 0)

    def parts(turn, which):
        for l in which:
            for k in range(members):
                hi, lo = split(ub[l, pl.ds(k * ext, ext), cols:2 * cols])
                p_ref[turn, k, l] = math.sqrt(ce2) * lon_pass(l, hi, lo, 1)

    def static_part(turn, send, recv):
        hi, lo = split(us[:, cols:2 * cols])
        ps_ref[turn, mem] = math.sqrt(cs2) * lon_pass(mem, hi, lo, 1)
        copies = []
        for o in range(1, n_mem):
            one = copy(
                ps_ref.at[turn, mem], ps_ref.at[turn, mem], send.at[o - 1], recv.at[o - 1], at(0, 0, o)
            )
            one.start()
            copies.append(one)
        return copies

    def scatter_sum(slots, send, recv):
        copies = []
        for o in range(1, n_mem):
            peer = lax.rem(mem + o, n_mem)
            one = copy(y_ref.at[peer], slots.at[o - 1], send.at[o - 1], recv.at[o - 1], at(0, 0, o))
            one.start()
            copies.append(one)
        return copies

    def finish_sum(copies, slots):
        for one in copies:
            one.wait()
        total = y_ref[mem]
        for o in range(n_mem - 1):
            total = total + slots[o]
        return total

    for number in range(CHUNKS):
        for one in a_copies[number]:
            one.wait_recv()
        apply_members(f0c, f0l, f0r, number * batch, batch)
        if number + 3 < CHUNKS:
            a_copies.append(send_chunk(number + 3))
    apply_static(f0c, f0l, f0r)
    r0_copies = scatter_sum(yr.at[0], r0_send, r0_recv)
    parts(0, (0, 1))
    y0 = finish_sum(r0_copies, yr.at[0])
    t0 = f0c[mem, own, :]
    t1 = obs[mem] * y0
    t1_ref[...] = t1
    f1c[mem, own, :] = t1
    g_copies = []
    for o in range(1, n_mem):
        one = copy(t1_ref, f1c.at[mem, own, :], g_send.at[o - 1], g_recv.at[o - 1], at(0, 0, o))
        one.start()
        g_copies.append(one)
    parts(0, (2, 3))
    for one in g_copies:
        one.wait_recv()
    pack(f1c, k1l, k1r)
    f1_copies = halo(f1c, f1l, f1r, k1l, k1r, f1_send, f1_recv)
    q0_copies = static_part(0, q0_send, q0_recv)
    for one in f1_copies:
        one.wait_recv()
    apply_members(f1c, f1l, f1r, 0, members)
    apply_static(f1c, f1l, f1r)
    r1_copies = scatter_sum(yr.at[1], r1_send, r1_recv)
    parts(1, range(levels))
    y1 = finish_sum(r1_copies, yr.at[1])

    def summed(x):
        return jnp.sum(jnp.sum(x, axis=0, keepdims=True), axis=1, keepdims=True)

    lane = iota((8, cols), 1)
    sums = jnp.zeros((8, cols), F32)
    for number, value in enumerate((t0 * y0, t1 * y0, t1 * y1, y1 * (obs[mem] * y1))):
        sums = jnp.where(lane == number, summed(value), sums)

    def total_start(value, slots, me, offsets, send, recv):
        slots[me] = value
        copies = []
        for number, offset in enumerate(offsets):
            one = copy(slots.at[me], slots.at[me], send.at[number], recv.at[number], at(*offset))
            one.start()
            copies.append(one)
        return copies

    def total_finish(slots, copies):
        for one in copies:
            one.wait_recv()
        out = slots[0]
        for other in range(1, len(copies) + 1):
            out = out + slots[other]
        return out

    plane_copies = total_start(sums, gather_plane, lat * n_mem + mem, plane, sp_send, sp_recv)
    sums = total_finish(gather_plane, plane_copies)
    line_copies = total_start(sums, gather_lon, lon, line, so_send, so_recv)
    q1_copies = static_part(1, q1_send, q1_recv)
    sums = total_finish(gather_lon, line_copies)
    row = sums[0:1]

    def pick(number):
        return jnp.sum(jnp.where(iota((1, cols), 1) == number, row, 0.0), axis=1, keepdims=True)

    rr = pick(0)
    u, v, s = pick(1) / rr, pick(2) / rr, pick(3) / rr
    alpha = 1.0 / (1.0 + u)
    beta = (v - u * u) * alpha * alpha
    g, h = 1.0 - alpha + beta, -alpha
    alpha_next = beta / (g * g * (1.0 + u) + 2.0 * g * h * (u + v) + h * h * (v + s))
    near, far = alpha + alpha_next * g, alpha_next * h
    outs = []
    for k in range(members):
        p_ref[0, k] = near * p_ref[0, k] + far * p_ref[1, k]
        outs.append(pltpu.make_async_copy(p_ref.at[0, k], ens_out.at[k], out_sem.at[k]))
        outs[-1].start()
    for one in q0_copies + q1_copies:
        one.wait()
    y_ref[...] = near * ps_ref[0] + far * ps_ref[1]
    outs.append(pltpu.make_async_copy(y_ref, static_out, out_sem.at[members]))
    outs[-1].start()
    for one in outs:
        one.wait()
    for copies in a_copies:
        for one in copies:
            one.wait_send()
    for one in f0_copies + g_copies + f1_copies + plane_copies + line_copies:
        one.wait_send()


def per_device(n_lon, n_lat, n_mem, anomalies, spread, obs_index, innovation, obs_weight, band_width):
    members, levels, rows, cols = anomalies.shape
    ext = rows + 2 * PAD
    count = obs_index.shape[-1]
    vmem, dma = pltpu.VMEM, pltpu.SemaphoreType.DMA
    dims = (n_lon, n_lat, n_mem, members, levels, rows, cols)
    far = pl.BlockSpec(memory_space=pltpu.HBM)
    return pl.pallas_call(
        lambda *refs: kernel(dims, *refs),
        out_shape=(
            jax.ShapeDtypeStruct((members, levels, rows, cols), F32),
            jax.ShapeDtypeStruct((levels, rows, cols), F32),
        ),
        in_specs=[far] * 6,
        out_specs=(far, far),
        scratch_shapes=[
            pltpu.SMEM((2, levels), jnp.int32),
            vmem((1, count), jnp.int32), vmem((1, count), F32), vmem((1, count), F32),
            vmem((members, levels, ext, cols), BF16),
            vmem((members, rows, cols), BF16), vmem((members, rows, cols), BF16),
            vmem((members, ext, cols), BF16), vmem((members, ext, cols), BF16),
            vmem((levels + 1, ext, cols), F32),
            vmem((1, rows, cols), F32), vmem((1, rows, cols), F32),
            vmem((1, ext, cols), F32), vmem((1, ext, cols), F32),
            vmem((levels, ext, cols), F32),
            vmem((1, rows, cols), F32), vmem((1, rows, cols), F32),
            vmem((1, ext, cols), F32), vmem((1, ext, cols), F32),
            vmem((levels, rows, cols), F32),
            vmem((levels, 9 * cols, 2 * cols), BF16),
            vmem((2, levels, 2 * rows, ext), BF16),
            vmem((levels, members * ext, 6 * cols), BF16),
            vmem((levels, members * ext, 2 * cols), F32),
            vmem((ext, 2 * cols), F32),
            vmem((2, members, levels, rows, cols), F32),
            vmem((2, levels, rows, cols), F32),
            vmem((2, ext, cols), F32),
            vmem((levels, rows, cols), F32),
            vmem((2, n_mem - 1, rows, cols), F32),
            vmem((rows, cols), F32),
            vmem((n_lat * n_mem, 8, cols), F32), vmem((n_lon, 8, cols), F32),
        ]
        + [dma((6,))]
        + [dma((CHUNKS, 8))] * 2
        + [dma((8,))] * 4
        + [dma((n_mem - 1,))] * 10
        + [dma((n_lat * n_mem - 1,))] * 2
        + [dma((n_lon - 1,))] * 2
        + [dma((members + 1,))],
        compiler_params=pltpu.CompilerParams(
            collective_id=0, has_side_effects=True, vmem_limit_bytes=63 * 1024 * 1024
        ),
    )(
        band_width, anomalies, spread, obs_index.reshape(1, count), innovation.reshape(1, count),
        obs_weight.reshape(1, count),
    )


def solution(mesh):
    n_lon, n_lat, n_mem = (mesh.shape[name] for name in ("lon", "lat", "mem"))
    return jax.shard_map(
        lambda *args: per_device(n_lon, n_lat, n_mem, *args),
        mesh=mesh,
        in_specs=(
            P("mem", None, "lon", "lat"),
            P(None, "lon", "lat"),
            P("lon", "lat", None),
            P("lon", "lat", None),
            P("lon", "lat", None),
            P(),
        ),
        out_specs=(P("mem", None, "lon", "lat"), P(None, "lon", "lat")),
        check_vma=False,
    )
```

time: 87 us -> 71 us (0.82)
  Pallas kernels: 76.3 us -> 67.2 us
  other arithmetic: 4.34 us -> 0 us
  local copies, waits for them, and re-layouts: 5.36 us -> 3 us
    pallas_call x1, Pallas kernels: 76.3 us -> 67.2 us  [per_device(): pl.pallas_call(lambda *refs: kernel(dims, *refs), out_shape=(jax.ShapeDty...]
    add x2 -> x0, other arithmetic: 4.34 us -> none  [the longest x1 2.43 us: per_device(): near * parts[0] + far * parts[1]]
    unnamed x12 -> x4, local copies, waits for them, and re-layouts: 4.71 us -> 3 us
where the time goes in v1:
time: 71 us; the launch traced here: 70.8 us
  Pallas kernels  67.2 us (95%)
  local copies, waits for them, and re-layouts  3 us (4%)
    pallas_call x1, Pallas kernels, per_device(): pl.pallas_call(lambda *refs: kernel(dims, *refs), out_shape=(jax.ShapeDty...  67.2 us
    unnamed x4, local copies, waits for them, and re-layouts  3 us

profile of v1, /device:TPU:1, one launch (start us, length us, event | category | flops | bytes accessed | tf_op | source)
XLA Modules:
  0.0 70.8 jit_solution(14324672009655980387)
XLA Ops:
  0.6 67.2 %shard_map.77 = (f32[8,4,64,128]{3,2,1,0:T(8,128)}, f32[4,64,128]{2,1,0:T(8,128)}) custom-call(s32[2,4]{1,0:T(2,128)} %refs_0_.1, bf16[8,4,64,128]{3,2,1,0:T(8,128)(2,1)} %refs_1_.1, f32[4,64,128]{2,1,0:T(8,128)} %refs_2_.1, s32[1,2048]{1,0:T(1,128)} %bitcast.3, f32[1,2048]{1,0:T(1,128)} %bitcast.4, f32[1,2048]{1,0:T(1,128)} %bitcast.5), custom_call_target="tpu_custom_call" | custom-call | tf_op jit(solution)/shard_map/pallas_call | solution.py:395
  67.8 0.0 copy-start
  67.8 2.3 %copy.10 = f32[8,4,64,128]{3,2,1,0:T(8,128)} copy(f32[8,4,64,128]{3,2,1,0:T(8,128)} %get-tuple-element.4) | data formatting | bytes 2097152
  70.2 0.0 copy-done
  70.2 0.7 copy.11
Async XLA Ops:
  67.8 2.4 %copy-start = (f32[4,64,128]{2,1,0:T(8,128)S(1)}, f32[4,64,128]{2,1,0:T(8,128)}, u32[]{:S(2)}) copy-start(f32[4,64,128]{2,1,0:T(8,128)} %get-tuple-element.5) | copy-start | bytes 393220

commit v2 on v1

--- a/solution.py
+++ b/solution.py
@@ -9,7 +9,7 @@
 
 BAND = 12
 HALO = 2 * BAND
-PAD = 32
+PAD = HALO
 CHUNKS = 4
 hybrid_ens = 0.75
 hybrid_static = 0.25
@@ -32,11 +32,11 @@
     return high, (x - high.astype(F32)).astype(BF16)
 
 
-def kernel(dims, band_any, a_any, s_any, idx_any, inn_any, wt_any, ens_out, static_out,
+def kernel(dims, band_any, a_any, s_any, idx_any, inn_any, wt_any, ens_out, static_out, lam_out,
            band_ref, idx_ref, inn_ref, wt_ref, ac, kl, kr, hl, hr, f0c, k0l, k0r, f0l, f0r, f1c, k1l, k1r, f1l, f1r,
-           obs, mlat, nlon, xs, ub, us, p_ref, ps_ref, sl, y_ref, yr, t1_ref, gather_plane, gather_lon,
+           obs, mlat, nlon, xs, ub, us, p_ref, ps_ref, lam_ref, sl, y_ref, yr, t1_ref, gather_plane, gather_lon,
            in_sem, a_send, a_recv, f0_send, f0_recv, f1_send, f1_recv, r0_send, r0_recv, r1_send, r1_recv,
-           g_send, g_recv, q0_send, q0_recv, q1_send, q1_recv, sp_send, sp_recv, so_send, so_recv, out_sem):
+           g_send, g_recv, c1_send, c1_recv, q0_send, q0_recv, q1_send, q1_recv, sp_send, sp_recv, so_send, so_recv, out_sem):
     n_lon, n_lat, n_mem, members, levels, rows, cols = dims
     lon, lat, mem = lax.axis_index("lon"), lax.axis_index("lat"), lax.axis_index("mem")
     ce2 = hybrid_ens / (members * n_mem)
@@ -54,10 +54,11 @@
         return pltpu.make_async_remote_copy(
             src_ref=src, dst_ref=dst, send_sem=send, recv_sem=recv, device_id=device, device_id_type=MESH
         )
-
-    plane = [(0, ol, om) for ol in range(n_lat) for om in range(n_mem) if (ol, om) != (0, 0)]
-    line = [(o, 0, 0) for o in range(1, n_lon)]
-    partners = sorted({(dx % n_lon, dy % n_lat, 0) for dx, dy in AROUND} | set(plane) | set(line))
+    parity = lax.rem(lon, 2)
+    across = 1 - 2 * parity
+    plane = [(tx * across, ol, om) for tx in range(2) for ol in range(n_lat) for om in range(n_mem)][1:]
+    line = [(o, 0, 0) for o in range(2, n_lon, 2)]
+    partners = plane + line + [(-across, dy, 0) for dy in (0, 1, -1)] + [(-across, 0, o) for o in range(1, n_mem)]
     barrier = pltpu.get_barrier_semaphore()
     for partner in partners:
         pl.semaphore_signal(barrier, inc=1, device_id=at(*partner), device_id_type=MESH)
@@ -74,7 +75,6 @@
         one.start()
     low, high = pl.ds(PAD - HALO, HALO), pl.ds(PAD + rows, HALO)
     first, last = pl.ds(0, HALO), pl.ds(rows - HALO, HALO)
-
     sel_row, sel_col = iota((levels * cols, 2 * cols), 0), iota((levels * cols, 2 * cols), 1)
     sel_level, sel_lat = sel_row // cols, lax.rem(sel_row, cols)
     spot = lax.rem(sel_col, cols) - HALO * sel_level
@@ -89,23 +89,15 @@
     ).astype(BF16)
     kl[...] = packed[:, :cols].reshape(members, rows, cols)
     kr[...] = packed[:, cols:].reshape(members, rows, cols)
-    edges = (pl.ds(0, PAD - HALO), pl.ds(PAD + rows + HALO, PAD - HALO))
-    for edge in edges:
-        ac[:, :, edge, :] = jnp.zeros((members, levels, PAD - HALO, cols), BF16)
-        for ref in (hl, hr):
-            ref[:, edge, :] = jnp.zeros((members, PAD - HALO, cols), BF16)
-        for ref in (f0c, f0l, f0r, f1c, f1l, f1r):
-            ref[:, edge, :] = jnp.zeros((ref.shape[0], PAD - HALO, cols), F32)
-
     pl.semaphore_wait(barrier, len(partners))
 
     from_rows = {1: last, -1: first, 0: pl.ds(0, rows)}
     field_rows = {1: pl.ds(PAD + rows - HALO, HALO), -1: pl.ds(PAD, HALO)}
     to_rows = {1: low, -1: high, 0: own}
 
-    def halo(centre, left, right, packed_left, packed_right, send, recv, chunk=None):
+    def halo(centre, left, right, packed_left, packed_right, send, recv, chunk=None, skip=0):
         copies = []
-        for number, (dx, dy) in enumerate(AROUND):
+        for number, (dx, dy) in enumerate(AROUND[skip:]):
             if dy == 0:
                 if chunk is None:
                     src, dst = centre.at[:, field_rows[dx], :], centre.at[:, to_rows[dx], :]
@@ -124,9 +116,7 @@
 
     def send_chunk(number):
         return halo(ac, hl, hr, kl, kr, a_send.at[number], a_recv.at[number], pl.ds(number * batch, batch))
-
     a_copies = [send_chunk(0)]
-
     index = idx_ref[...]
     weight = wt_ref[...]
     at_row, at_col = index // cols, lax.rem(index, cols)
@@ -150,8 +140,15 @@
 
     lax.fori_loop(0, levels, level_fields, 0)
 
+    select16 = select.astype(BF16)
+
+    def select_exact(x, chosen):
+        terms = dot(jnp.concatenate([t.astype(BF16) for t in thirds(x)], axis=0), chosen)
+        return terms[0:rows] + terms[rows:2 * rows] + terms[2 * rows:]
+
     def pack(centre, left, right, extra=0.0):
-        both = dot(jnp.concatenate([centre[l, own, :] for l in range(levels)], axis=1), select, HI) + extra
+        whole = jnp.concatenate([centre[l, own, :] for l in range(levels)], axis=1)
+        both = select_exact(whole, select16) + extra
         left[0] = both[:, :cols]
         right[0] = both[:, cols:]
 
@@ -159,7 +156,7 @@
     spot = lax.rem(iota((cols, 2 * cols), 1), cols) - spare
     wanted = jnp.where(iota((cols, 2 * cols), 1) < cols, spot + (cols - HALO), spot)
     place = jnp.where((spot >= 0) & (spot < HALO) & (iota((cols, 2 * cols), 0) == wanted), 1.0, 0.0)
-    pack(f0c, k0l, k0r, dot(f0c[levels, own, :], place, HI))
+    pack(f0c, k0l, k0r, select_exact(f0c[levels, own, :], place.astype(BF16)))
     f0_copies = halo(f0c, f0l, f0r, k0l, k0r, f0_send, f0_recv)
     a_copies.append(send_chunk(1))
     r, c = iota((cols, cols), 0), iota((cols, cols), 1)
@@ -207,10 +204,10 @@
         return carry
 
     lax.fori_loop(0, levels, level_matrices, 0)
-
+    a_copies.append(send_chunk(2))
     for one in f0_copies:
         one.wait_recv()
-    a_copies.append(send_chunk(2))
+    a_copies.append(send_chunk(3))
     realign = jnp.where((r - spare == c - HALO * mem) & (r >= spare) & (r < spare + HALO), 1.0, 0.0)
     sl[0] = dot(f0l[0], realign, HI)
     sl[1] = dot(f0r[0], realign, HI)
@@ -234,16 +231,22 @@
                 hi, lo = split(ac[k, l].astype(F32) * z[l])
                 xs[l, spans, 0:cols] = hi
                 xs[l, spans, 3 * cols:4 * cols] = lo
-        for l in range(levels):
+        def lat_level(l):
             ub[l, chunk, :] = dot(xs[l, chunk, :], mlat[l, 0:6 * cols, :]) + dot(
                 xs[l, chunk, 0:3 * cols], mlat[l, 6 * cols:, :]
             )
-        for l in range(levels):
+
+        def lon_level(l):
             total = jnp.zeros((rows, cols), F32)
             for k in range(start, start + count):
                 hi, lo = split(ub[l, pl.ds(k * ext, ext), 0:cols])
                 total += ac[k, l, own, :].astype(F32) * lon_pass(l, hi, lo, 0)
             y_ref[l] = ce2 * total if start == 0 else y_ref[l] + ce2 * total
+
+        for l in range(levels):
+            lat_level(l)
+        for l in range(levels):
+            lon_level(l)
 
     def apply_static(centre, left, right):
         his, los = [], []
@@ -277,17 +280,16 @@
     def scatter_sum(slots, send, recv):
         copies = []
         for o in range(1, n_mem):
-            peer = lax.rem(mem + o, n_mem)
-            one = copy(y_ref.at[peer], slots.at[o - 1], send.at[o - 1], recv.at[o - 1], at(0, 0, o))
+            other = lax.rem(mem + o, n_mem)
+            one = copy(y_ref.at[other], slots.at[o - 1], send.at[o - 1], recv.at[o - 1], at(0, 0, o))
             one.start()
             copies.append(one)
         return copies
 
     def finish_sum(copies, slots):
-        for one in copies:
+        total = y_ref[mem]
+        for o, one in enumerate(copies):
             one.wait()
-        total = y_ref[mem]
-        for o in range(n_mem - 1):
             total = total + slots[o]
         return total
 
@@ -295,33 +297,43 @@
         for one in a_copies[number]:
             one.wait_recv()
         apply_members(f0c, f0l, f0r, number * batch, batch)
-        if number + 3 < CHUNKS:
-            a_copies.append(send_chunk(number + 3))
+    r0_copies = scatter_sum(yr.at[0], r0_send, r0_recv)
     apply_static(f0c, f0l, f0r)
-    r0_copies = scatter_sum(yr.at[0], r0_send, r0_recv)
     parts(0, (0, 1))
     y0 = finish_sum(r0_copies, yr.at[0])
     t0 = f0c[mem, own, :]
     t1 = obs[mem] * y0
     t1_ref[...] = t1
     f1c[mem, own, :] = t1
-    g_copies = []
+    g_copies, c1_copies = [], []
     for o in range(1, n_mem):
         one = copy(t1_ref, f1c.at[mem, own, :], g_send.at[o - 1], g_recv.at[o - 1], at(0, 0, o))
         one.start()
         g_copies.append(one)
+    for number, dx in enumerate((1, -1)):
+        for o in range(n_mem):
+            one = copy(
+                t1_ref.at[from_rows[dx], :], f1c.at[mem, to_rows[dx], :],
+                c1_send.at[number, o], c1_recv.at[number, o], at(dx, 0, o),
+            )
+            one.start()
+            c1_copies.append(one)
     parts(0, (2, 3))
+    outs = [pltpu.make_async_copy(p_ref.at[0], ens_out.at[0], out_sem.at[0])]
+    outs[-1].start()
     for one in g_copies:
         one.wait_recv()
     pack(f1c, k1l, k1r)
-    f1_copies = halo(f1c, f1l, f1r, k1l, k1r, f1_send, f1_recv)
+    f1_copies = halo(f1c, f1l, f1r, k1l, k1r, f1_send, f1_recv, skip=2)
     q0_copies = static_part(0, q0_send, q0_recv)
-    for one in f1_copies:
+    for one in f1_copies + c1_copies:
         one.wait_recv()
     apply_members(f1c, f1l, f1r, 0, members)
+    r1_copies = scatter_sum(yr.at[1], r1_send, r1_recv)
     apply_static(f1c, f1l, f1r)
-    r1_copies = scatter_sum(yr.at[1], r1_send, r1_recv)
     parts(1, range(levels))
+    outs.append(pltpu.make_async_copy(p_ref.at[1], ens_out.at[1], out_sem.at[1]))
+    outs[-1].start()
     y1 = finish_sum(r1_copies, yr.at[1])
 
     def summed(x):
@@ -336,7 +348,7 @@
         slots[me] = value
         copies = []
         for number, offset in enumerate(offsets):
-            one = copy(slots.at[me], slots.at[me], send.at[number], recv.at[number], at(*offset))
+            one = copy(slots.at[me, 0:1, :], slots.at[me, 0:1, :], send.at[number], recv.at[number], at(*offset))
             one.start()
             copies.append(one)
         return copies
@@ -344,14 +356,14 @@
     def total_finish(slots, copies):
         for one in copies:
             one.wait_recv()
-        out = slots[0]
+        out = slots[0, 0:1, :]
         for other in range(1, len(copies) + 1):
-            out = out + slots[other]
-        return out
-
-    plane_copies = total_start(sums, gather_plane, lat * n_mem + mem, plane, sp_send, sp_recv)
+            out = out + slots[other, 0:1, :]
+        return jnp.broadcast_to(out, (8, cols))
+
+    plane_copies = total_start(sums, gather_plane, (parity * n_lat + lat) * n_mem + mem, plane, sp_send, sp_recv)
     sums = total_finish(gather_plane, plane_copies)
-    line_copies = total_start(sums, gather_lon, lon, line, so_send, so_recv)
+    line_copies = total_start(sums, gather_lon, lon // 2, line, so_send, so_recv)
     q1_copies = static_part(1, q1_send, q1_recv)
     sums = total_finish(gather_lon, line_copies)
     row = sums[0:1]
@@ -365,24 +377,45 @@
     beta = (v - u * u) * alpha * alpha
     g, h = 1.0 - alpha + beta, -alpha
     alpha_next = beta / (g * g * (1.0 + u) + 2.0 * g * h * (u + v) + h * h * (v + s))
-    near, far = alpha + alpha_next * g, alpha_next * h
-    outs = []
-    for k in range(members):
-        p_ref[0, k] = near * p_ref[0, k] + far * p_ref[1, k]
-        outs.append(pltpu.make_async_copy(p_ref.at[0, k], ens_out.at[k], out_sem.at[k]))
-        outs[-1].start()
+    lam_ref[...] = jnp.where(lane == 0, alpha + alpha_next * g, alpha_next * h)
+    outs.append(pltpu.make_async_copy(lam_ref, lam_out, out_sem.at[2]))
+    outs[-1].start()
     for one in q0_copies + q1_copies:
         one.wait()
-    y_ref[...] = near * ps_ref[0] + far * ps_ref[1]
-    outs.append(pltpu.make_async_copy(y_ref, static_out, out_sem.at[members]))
+    outs.append(pltpu.make_async_copy(ps_ref, static_out, out_sem.at[3]))
     outs[-1].start()
     for one in outs:
         one.wait()
     for copies in a_copies:
         for one in copies:
             one.wait_send()
-    for one in f0_copies + g_copies + f1_copies + plane_copies + line_copies:
+    for one in f0_copies + g_copies + c1_copies + f1_copies + plane_copies + line_copies:
         one.wait_send()
+
+
+def combine(ens_in, static_in, lam_in, ens_out, static_out, ens, static, lam, ens_sem, in_sem, out_sem):
+    members = ens_out.shape[0]
+    lam_copy = pltpu.make_async_copy(lam_in, lam, in_sem.at[0])
+    static_copy = pltpu.make_async_copy(static_in, static, in_sem.at[1])
+    lam_copy.start()
+    loads = [pltpu.make_async_copy(ens_in.at[:, k], ens.at[:, k], ens_sem.at[k]) for k in range(members)]
+    for one in loads:
+        one.start()
+    static_copy.start()
+    lam_copy.wait()
+    near, far = lam[0:1, 0:1], lam[0:1, 1:2]
+    stores = []
+    for k in range(members):
+        loads[k].wait()
+        ens[0, k] = near * ens[0, k] + far * ens[1, k]
+        stores.append(pltpu.make_async_copy(ens.at[0, k], ens_out.at[k], out_sem.at[k]))
+        stores[-1].start()
+    static_copy.wait()
+    static[0] = near * static[0] + far * static[1]
+    stores.append(pltpu.make_async_copy(static.at[0], static_out, out_sem.at[members]))
+    stores[-1].start()
+    for one in stores:
+        one.wait()
 
 
 def per_device(n_lon, n_lat, n_mem, anomalies, spread, obs_index, innovation, obs_weight, band_width):
@@ -392,14 +425,15 @@
     vmem, dma = pltpu.VMEM, pltpu.SemaphoreType.DMA
     dims = (n_lon, n_lat, n_mem, members, levels, rows, cols)
     far = pl.BlockSpec(memory_space=pltpu.HBM)
-    return pl.pallas_call(
+    done = pl.pallas_call(
         lambda *refs: kernel(dims, *refs),
         out_shape=(
-            jax.ShapeDtypeStruct((members, levels, rows, cols), F32),
-            jax.ShapeDtypeStruct((levels, rows, cols), F32),
+            jax.ShapeDtypeStruct((2, members, levels, rows, cols), F32),
+            jax.ShapeDtypeStruct((2, levels, rows, cols), F32),
+            jax.ShapeDtypeStruct((8, cols), F32),
         ),
         in_specs=[far] * 6,
-        out_specs=(far, far),
+        out_specs=(far, far, far),
         scratch_shapes=[
             pltpu.SMEM((2, levels), jnp.int32),
             vmem((1, count), jnp.int32), vmem((1, count), F32), vmem((1, count), F32),
@@ -420,19 +454,23 @@
             vmem((ext, 2 * cols), F32),
             vmem((2, members, levels, rows, cols), F32),
             vmem((2, levels, rows, cols), F32),
+            vmem((8, cols), F32),
             vmem((2, ext, cols), F32),
             vmem((levels, rows, cols), F32),
             vmem((2, n_mem - 1, rows, cols), F32),
             vmem((rows, cols), F32),
-            vmem((n_lat * n_mem, 8, cols), F32), vmem((n_lon, 8, cols), F32),
+            vmem((2 * n_lat * n_mem, 8, cols), F32), vmem((n_lon // 2, 8, cols), F32),
         ]
         + [dma((6,))]
         + [dma((CHUNKS, 8))] * 2
         + [dma((8,))] * 4
-        + [dma((n_mem - 1,))] * 10
-        + [dma((n_lat * n_mem - 1,))] * 2
-        + [dma((n_lon - 1,))] * 2
-        + [dma((members + 1,))],
+        + [dma((n_mem - 1,))] * 4
+        + [dma((n_mem - 1,))] * 2
+        + [dma((2, n_mem))] * 2
+        + [dma((n_mem - 1,))] * 4
+        + [dma((2 * n_lat * n_mem - 1,))] * 2
+        + [dma((n_lon // 2 - 1,))] * 2
+        + [dma((4,))],
         compiler_params=pltpu.CompilerParams(
             collective_id=0, has_side_effects=True, vmem_limit_bytes=63 * 1024 * 1024
         ),
@@ -440,6 +478,20 @@
         band_width, anomalies, spread, obs_index.reshape(1, count), innovation.reshape(1, count),
         obs_weight.reshape(1, count),
     )
+    return pl.pallas_call(
+        combine,
+        out_shape=(
+            jax.ShapeDtypeStruct((members, levels, rows, cols), F32),
+            jax.ShapeDtypeStruct((levels, rows, cols), F32),
+        ),
+        in_specs=[far] * 3,
+        out_specs=(far, far),
+        scratch_shapes=[
+            vmem((2, members, levels, rows, cols), F32), vmem((2, levels, rows, cols), F32), vmem((8, cols), F32),
+            dma((members,)), dma((2,)), dma((members + 1,)),
+        ],
+        compiler_params=pltpu.CompilerParams(vmem_limit_bytes=63 * 1024 * 1024),
+    )(*done)
 
 
 def solution(mesh):

time: 71 us -> 65.6 us (0.924)
  local copies, waits for them, and re-layouts: 3 us -> 0 us
  Pallas kernels: 67.2 us -> 64.8 us
    pallas_call x1, Pallas kernels: 67.2 us -> 62.3 us  [per_device(): pl.pallas_call(lambda *refs: kernel(dims, *refs), out_shape=(jax.ShapeDty...]
    unnamed x4 -> x0, local copies, waits for them, and re-layouts: 3 us -> none
    pallas_call x0 -> x1, Pallas kernels: none -> 2.53 us  [per_device(): pl.pallas_call(combine, out_shape=(jax.ShapeDtypeStruct((members, levels,...]
where the time goes in v2:
time: 65.6 us; the launch traced here: 65.4 us
  Pallas kernels  64.8 us (99%)
    pallas_call x1, Pallas kernels, per_device(): pl.pallas_call(lambda *refs: kernel(dims, *refs), out_shape=(jax.ShapeDty...  62.3 us
    pallas_call x1, Pallas kernels, per_device(): pl.pallas_call(combine, out_shape=(jax.ShapeDtypeStruct((members, levels,...  2.53 us

profile of v2, /device:TPU:1, one launch (start us, length us, event | category | flops | bytes accessed | tf_op | source)
XLA Modules:
  0.0 65.4 jit_solution(5461629856430030669)
XLA Ops:
  0.6 62.3 %shard_map.77 = (f32[2,8,4,64,128]{4,3,2,1,0:T(8,128)}, f32[2,4,64,128]{3,2,1,0:T(8,128)}, f32[8,128]{1,0:T(8,128)}) custom-call(s32[2,4]{1,0:T(2,128)} %refs_0_.1, bf16[8,4,64,128]{3,2,1,0:T(8,128)(2,1)} %refs_1_.1, f32[4,64,128]{2,1,0:T(8,128)} %refs_2_.1, s32[1,2048]{1,0:T(1,128)} %bitcast.3, f32[1,2048]{1,0:T(1,128)} %bitcast.4, f32[1,2048]{1,0:T(1,128)} %bitcast.5), custom_call_target="tpu_custom_call" | custom-call | tf_op jit(solution)/shard_map/pallas_call | solution.py:428
  62.9 2.5 %shard_map.78 = (f32[8,4,64,128]{3,2,1,0:T(8,128)}, f32[4,64,128]{2,1,0:T(8,128)}) custom-call(f32[2,8,4,64,128]{4,3,2,1,0:T(8,128)} %get-tuple-element.5.ens_in, f32[2,4,64,128]{3,2,1,0:T(8,128)} %get-tuple-element.6.static_in, f32[8,128]{1,0:T(8,128)} %get-tuple-element.7.lam_in), custom_call_target="tpu_custom_call" | custom-call | tf_op jit(solution)/shard_map/pallas_call | solution.py:481

commit v3 on v2

--- a/solution.py
+++ b/solution.py
@@ -9,7 +9,6 @@
 
 BAND = 12
 HALO = 2 * BAND
-PAD = HALO
 CHUNKS = 4
 hybrid_ens = 0.75
 hybrid_static = 0.25
@@ -34,14 +33,14 @@
 
 def kernel(dims, band_any, a_any, s_any, idx_any, inn_any, wt_any, ens_out, static_out, lam_out,
            band_ref, idx_ref, inn_ref, wt_ref, ac, kl, kr, hl, hr, f0c, k0l, k0r, f0l, f0r, f1c, k1l, k1r, f1l, f1r,
-           obs, mlat, nlon, xs, ub, us, p_ref, ps_ref, lam_ref, sl, y_ref, yr, t1_ref, gather_plane, gather_lon,
-           in_sem, a_send, a_recv, f0_send, f0_recv, f1_send, f1_recv, r0_send, r0_recv, r1_send, r1_recv,
+           obs, mlat, nlon, nrim, xs, ub, us, p_ref, ps_ref, lam_ref, sl, y_ref, yr, t1_ref, gather_plane, gather_lon,
+           in_sem, a_send, a_recv, f0_send, f0_recv, z_send, z_recv, f1_send, f1_recv, r0_send, r0_recv, r1_send, r1_recv,
            g_send, g_recv, c1_send, c1_recv, q0_send, q0_recv, q1_send, q1_recv, sp_send, sp_recv, so_send, so_recv, out_sem):
     n_lon, n_lat, n_mem, members, levels, rows, cols = dims
     lon, lat, mem = lax.axis_index("lon"), lax.axis_index("lat"), lax.axis_index("mem")
     ce2 = hybrid_ens / (members * n_mem)
     cs2 = hybrid_static
-    ext = rows + 2 * PAD
+    ext = rows + 2 * HALO
 
     def at(dlon=0, dlat=0, dmem=0):
         return {
@@ -63,7 +62,7 @@
     for partner in partners:
         pl.semaphore_signal(barrier, inc=1, device_id=at(*partner), device_id_type=MESH)
 
-    own = pl.ds(PAD, rows)
+    own = pl.ds(0, rows)
     inputs = [
         pltpu.make_async_copy(src, dst, in_sem.at[number])
         for number, (src, dst) in enumerate((
@@ -73,7 +72,7 @@
     ]
     for one in inputs:
         one.start()
-    low, high = pl.ds(PAD - HALO, HALO), pl.ds(PAD + rows, HALO)
+    low, high = pl.ds(rows, HALO), pl.ds(rows + HALO, HALO)
     first, last = pl.ds(0, HALO), pl.ds(rows - HALO, HALO)
     sel_row, sel_col = iota((levels * cols, 2 * cols), 0), iota((levels * cols, 2 * cols), 1)
     sel_level, sel_lat = sel_row // cols, lax.rem(sel_row, cols)
@@ -92,7 +91,6 @@
     pl.semaphore_wait(barrier, len(partners))
 
     from_rows = {1: last, -1: first, 0: pl.ds(0, rows)}
-    field_rows = {1: pl.ds(PAD + rows - HALO, HALO), -1: pl.ds(PAD, HALO)}
     to_rows = {1: low, -1: high, 0: own}
 
     def halo(centre, left, right, packed_left, packed_right, send, recv, chunk=None, skip=0):
@@ -100,9 +98,9 @@
         for number, (dx, dy) in enumerate(AROUND[skip:]):
             if dy == 0:
                 if chunk is None:
-                    src, dst = centre.at[:, field_rows[dx], :], centre.at[:, to_rows[dx], :]
+                    src, dst = centre.at[:, from_rows[dx], :], centre.at[:, to_rows[dx], :]
                 else:
-                    src, dst = centre.at[chunk, :, field_rows[dx], :], centre.at[chunk, :, to_rows[dx], :]
+                    src, dst = centre.at[chunk, :, from_rows[dx], :], centre.at[chunk, :, to_rows[dx], :]
             else:
                 every = slice(None) if chunk is None else chunk
                 src = (packed_left if dy == 1 else packed_right).at[every, from_rows[dx], :]
@@ -157,12 +155,27 @@
     wanted = jnp.where(iota((cols, 2 * cols), 1) < cols, spot + (cols - HALO), spot)
     place = jnp.where((spot >= 0) & (spot < HALO) & (iota((cols, 2 * cols), 0) == wanted), 1.0, 0.0)
     pack(f0c, k0l, k0r, select_exact(f0c[levels, own, :], place.astype(BF16)))
-    f0_copies = halo(f0c, f0l, f0r, k0l, k0r, f0_send, f0_recv)
+    half = levels // 2
+    ours = pl.ds(half * lax.rem(mem, 2), half)
+    twin = 1 - 2 * lax.rem(mem, 2)
+    z_copies, s_copies = [], []
+    for number, dx in enumerate((1, -1)):
+        for kind, (some, group) in enumerate(((ours, z_copies), (pl.ds(levels, 1), s_copies))):
+            one = copy(
+                f0c.at[some, from_rows[dx], :], f0c.at[some, to_rows[dx], :],
+                z_send.at[2 * kind + number], z_recv.at[2 * kind + number], at(dx, 0, 0),
+            )
+            one.start()
+            group.append(one)
+    f0_copies = s_copies + halo(f0c, f0l, f0r, k0l, k0r, f0_send, f0_recv, skip=2)
     a_copies.append(send_chunk(1))
     r, c = iota((cols, cols), 0), iota((cols, cols), 1)
     inside_low = jnp.where(lat > 0, 1.0, 0.0).astype(F32)
     inside_high = jnp.where(lat < n_lat - 1, 1.0, 0.0).astype(F32)
     offsets = iota((8, cols), 1) - BAND
+
+    def spot_of(row):
+        return jnp.where(row < rows, row, jnp.where(row < rows + HALO, row - rows - HALO, row - HALO))
 
     def level_matrices(l, carry):
         def band_of(which):
@@ -195,16 +208,26 @@
             mlat[l, (3 + part) * cols:(4 + part) * cols, :] = hi
             mlat[l, (6 + part) * cols:(7 + part) * cols, :] = lo
         band = band_of(0)
-        near = band(iota((rows, ext), 0) + PAD - iota((rows, ext), 1))
-        far = band(iota((ext, ext), 0) - iota((ext, ext), 1))
+        near = band(iota((rows, ext), 0) - spot_of(iota((rows, ext), 1)))
+        far = band(spot_of(iota((ext, ext), 0)) - spot_of(iota((ext, ext), 1)))
         for which, matrix in enumerate((dot(near, far, HI), near)):
             hi, lo = split(matrix)
             nlon[which, l, 0:rows, :] = hi
             nlon[which, l, rows:2 * rows, :] = lo
+            nrim[which, l, 0:rows, :] = hi[:, rows:]
+            nrim[which, l, rows:2 * rows, :] = lo[:, rows:]
         return carry
 
     lax.fori_loop(0, levels, level_matrices, 0)
     a_copies.append(send_chunk(2))
+    for number, (one, rim) in enumerate(zip(z_copies, (low, high))):
+        one.wait_recv()
+        passed = copy(
+            f0c.at[ours, rim, :], f0c.at[ours, rim, :],
+            z_send.at[4 + number], z_recv.at[4 + number], at(0, 0, twin),
+        )
+        passed.start()
+        f0_copies.append(passed)
     for one in f0_copies:
         one.wait_recv()
     a_copies.append(send_chunk(3))
@@ -212,41 +235,43 @@
     sl[0] = dot(f0l[0], realign, HI)
     sl[1] = dot(f0r[0], realign, HI)
 
-    def lon_pass(l, u_hi, u_lo, which):
-        tall = dot(nlon[which, l], u_hi)
-        return tall[0:rows] + tall[rows:] + dot(nlon[which, l, 0:rows, :], u_lo)
-
-    def apply_members(centre, left, right, start, count):
-        zl, zr = left[0], right[0]
-        z = [centre[l] for l in range(levels)]
-        chunk = pl.ds(start * ext, count * ext)
+    def lon_pass(l, u_hi, u_lo, which, matrix=nlon):
+        depth = u_hi.shape[0]
+        both = matrix[which, l] if matrix.shape[3] == depth else matrix[which, l, :, 0:depth]
+        tall = dot(both, u_hi)
+        return tall[0:rows] + tall[rows:] + dot(both[0:rows], u_lo)
+
+    every_row = (0, ext, 0)
+    own_rows, rim_rows = (0, rows, 0), (rows, 2 * HALO, members * rows)
+
+    def apply_members(centre, left, right, start, count, part, fresh):
+        row, size, base = part
+        some = pl.ds(row, size)
+        zl, zr = left[0, some, :], right[0, some, :]
+        z = [centre[l, some, :] for l in range(levels)]
+        chunk = pl.ds(base + start * size, count * size)
         for k in range(start, start + count):
-            spans = pl.ds(k * ext, ext)
-            for part, (rim, zz) in enumerate(((hl, zl), (hr, zr))):
-                hi, lo = split(rim[k].astype(F32) * zz)
+            spans = pl.ds(base + k * size, size)
+            for side, (rim, zz) in enumerate(((hl, zl), (hr, zr))):
+                hi, lo = split(rim[k, some, :].astype(F32) * zz)
                 for l in range(levels):
-                    xs[l, spans, (1 + part) * cols:(2 + part) * cols] = hi
-                    xs[l, spans, (4 + part) * cols:(5 + part) * cols] = lo
+                    xs[l, spans, (1 + side) * cols:(2 + side) * cols] = hi
+                    xs[l, spans, (4 + side) * cols:(5 + side) * cols] = lo
             for l in range(levels):
-                hi, lo = split(ac[k, l].astype(F32) * z[l])
+                hi, lo = split(ac[k, l, some, :].astype(F32) * z[l])
                 xs[l, spans, 0:cols] = hi
                 xs[l, spans, 3 * cols:4 * cols] = lo
-        def lat_level(l):
+        for l in range(levels):
             ub[l, chunk, :] = dot(xs[l, chunk, :], mlat[l, 0:6 * cols, :]) + dot(
                 xs[l, chunk, 0:3 * cols], mlat[l, 6 * cols:, :]
             )
-
-        def lon_level(l):
+        for l in range(levels):
             total = jnp.zeros((rows, cols), F32)
             for k in range(start, start + count):
-                hi, lo = split(ub[l, pl.ds(k * ext, ext), 0:cols])
-                total += ac[k, l, own, :].astype(F32) * lon_pass(l, hi, lo, 0)
-            y_ref[l] = ce2 * total if start == 0 else y_ref[l] + ce2 * total
-
-        for l in range(levels):
-            lat_level(l)
-        for l in range(levels):
-            lon_level(l)
+                hi, lo = split(ub[l, pl.ds(base + k * size, size), 0:cols])
+                part_sum = lon_pass(l, hi, lo, 0, nrim if row else nlon)
+                total += ac[k, l, own, :].astype(F32) * part_sum
+            y_ref[l] = ce2 * total if fresh else y_ref[l] + ce2 * total
 
     def apply_static(centre, left, right):
         his, los = [], []
@@ -262,7 +287,14 @@
     def parts(turn, which):
         for l in which:
             for k in range(members):
-                hi, lo = split(ub[l, pl.ds(k * ext, ext), cols:2 * cols])
+                if turn == 0:
+                    u = ub[l, pl.ds(k * ext, ext), cols:2 * cols]
+                else:
+                    u = jnp.concatenate(
+                        [ub[l, pl.ds(base + k * size, size), cols:2 * cols] for _, size, base in (own_rows, rim_rows)],
+                        axis=0,
+                    )
+                hi, lo = split(u)
                 p_ref[turn, k, l] = math.sqrt(ce2) * lon_pass(l, hi, lo, 1)
 
     def static_part(turn, send, recv):
@@ -296,7 +328,7 @@
     for number in range(CHUNKS):
         for one in a_copies[number]:
             one.wait_recv()
-        apply_members(f0c, f0l, f0r, number * batch, batch)
+        apply_members(f0c, f0l, f0r, number * batch, batch, every_row, number == 0)
     r0_copies = scatter_sum(yr.at[0], r0_send, r0_recv)
     apply_static(f0c, f0l, f0r)
     parts(0, (0, 1))
@@ -310,6 +342,15 @@
         one = copy(t1_ref, f1c.at[mem, own, :], g_send.at[o - 1], g_recv.at[o - 1], at(0, 0, o))
         one.start()
         g_copies.append(one)
+    parts(0, (2, 3))
+    outs = [pltpu.make_async_copy(p_ref.at[0], ens_out.at[0], out_sem.at[0])]
+    outs[-1].start()
+    for one in g_copies:
+        one.wait_recv()
+    pack(f1c, k1l, k1r)
+    f1_copies = halo(f1c, f1l, f1r, k1l, k1r, f1_send, f1_recv, skip=2)
+    f1_lat = [one for one, (dx, dy) in zip(f1_copies, AROUND[2:]) if dx == 0]
+    f1_corners = [one for one, (dx, dy) in zip(f1_copies, AROUND[2:]) if dx != 0]
     for number, dx in enumerate((1, -1)):
         for o in range(n_mem):
             one = copy(
@@ -318,17 +359,13 @@
             )
             one.start()
             c1_copies.append(one)
-    parts(0, (2, 3))
-    outs = [pltpu.make_async_copy(p_ref.at[0], ens_out.at[0], out_sem.at[0])]
-    outs[-1].start()
-    for one in g_copies:
+    for one in f1_lat:
         one.wait_recv()
-    pack(f1c, k1l, k1r)
-    f1_copies = halo(f1c, f1l, f1r, k1l, k1r, f1_send, f1_recv, skip=2)
+    apply_members(f1c, f1l, f1r, 0, members, own_rows, True)
+    for one in f1_corners + c1_copies:
+        one.wait_recv()
     q0_copies = static_part(0, q0_send, q0_recv)
-    for one in f1_copies + c1_copies:
-        one.wait_recv()
-    apply_members(f1c, f1l, f1r, 0, members)
+    apply_members(f1c, f1l, f1r, 0, members, rim_rows, False)
     r1_copies = scatter_sum(yr.at[1], r1_send, r1_recv)
     apply_static(f1c, f1l, f1r)
     parts(1, range(levels))
@@ -389,7 +426,7 @@
     for copies in a_copies:
         for one in copies:
             one.wait_send()
-    for one in f0_copies + g_copies + c1_copies + f1_copies + plane_copies + line_copies:
+    for one in z_copies + f0_copies + g_copies + c1_copies + f1_copies + plane_copies + line_copies:
         one.wait_send()
 
 
@@ -420,7 +457,7 @@
 
 def per_device(n_lon, n_lat, n_mem, anomalies, spread, obs_index, innovation, obs_weight, band_width):
     members, levels, rows, cols = anomalies.shape
-    ext = rows + 2 * PAD
+    ext = rows + 2 * HALO
     count = obs_index.shape[-1]
     vmem, dma = pltpu.VMEM, pltpu.SemaphoreType.DMA
     dims = (n_lon, n_lat, n_mem, members, levels, rows, cols)
@@ -449,6 +486,7 @@
             vmem((levels, rows, cols), F32),
             vmem((levels, 9 * cols, 2 * cols), BF16),
             vmem((2, levels, 2 * rows, ext), BF16),
+            vmem((2, levels, 2 * rows, 2 * HALO), BF16),
             vmem((levels, members * ext, 6 * cols), BF16),
             vmem((levels, members * ext, 2 * cols), F32),
             vmem((ext, 2 * cols), F32),
@@ -463,7 +501,9 @@
         ]
         + [dma((6,))]
         + [dma((CHUNKS, 8))] * 2
-        + [dma((8,))] * 4
+        + [dma((8,))] * 2
+        + [dma((6,))] * 2
+        + [dma((8,))] * 2
         + [dma((n_mem - 1,))] * 4
         + [dma((n_mem - 1,))] * 2
         + [dma((2, n_mem))] * 2

time: 65.6 us -> 63.3 us (0.965)
  Pallas kernels: 64.8 us -> 62.5 us
    pallas_call x1, Pallas kernels: 62.3 us -> 60 us  [per_device(): pl.pallas_call(lambda *refs: kernel(dims, *refs), out_shape=(jax.ShapeDty...]
where the time goes in v3:
time: 63.3 us; the launch traced here: 63.1 us
  Pallas kernels  62.5 us (99%)
  between operations  0.64 us (1%)
    pallas_call x1, Pallas kernels, per_device(): pl.pallas_call(lambda *refs: kernel(dims, *refs), out_shape=(jax.ShapeDty...  60 us
    pallas_call x1, Pallas kernels, per_device(): pl.pallas_call(combine, out_shape=(jax.ShapeDtypeStruct((members, levels,...  2.53 us

profile of v3, /device:TPU:1, one launch (start us, length us, event | category | flops | bytes accessed | tf_op | source)
XLA Modules:
  0.0 63.1 jit_solution(16482216690887804983)
XLA Ops:
  0.6 60.0 %shard_map.77 = (f32[2,8,4,64,128]{4,3,2,1,0:T(8,128)}, f32[2,4,64,128]{3,2,1,0:T(8,128)}, f32[8,128]{1,0:T(8,128)}) custom-call(s32[2,4]{1,0:T(2,128)} %refs_0_.1, bf16[8,4,64,128]{3,2,1,0:T(8,128)(2,1)} %refs_1_.1, f32[4,64,128]{2,1,0:T(8,128)} %refs_2_.1, s32[1,2048]{1,0:T(1,128)} %bitcast.3, f32[1,2048]{1,0:T(1,128)} %bitcast.4, f32[1,2048]{1,0:T(1,128)} %bitcast.5), custom_call_target="tpu_custom_call" | custom-call | tf_op jit(solution)/shard_map/pallas_call | solution.py:465
  60.6 2.5 %shard_map.78 = (f32[8,4,64,128]{3,2,1,0:T(8,128)}, f32[4,64,128]{2,1,0:T(8,128)}) custom-call(f32[2,8,4,64,128]{4,3,2,1,0:T(8,128)} %get-tuple-element.5.ens_in, f32[2,4,64,128]{3,2,1,0:T(8,128)} %get-tuple-element.6.static_in, f32[8,128]{1,0:T(8,128)} %get-tuple-element.7.lam_in), custom_call_target="tpu_custom_call" | custom-call | tf_op jit(solution)/shard_map/pallas_call | solution.py:521

commit v4 on v3

--- a/solution.py
+++ b/solution.py
@@ -93,9 +93,11 @@
     from_rows = {1: last, -1: first, 0: pl.ds(0, rows)}
     to_rows = {1: low, -1: high, 0: own}
 
-    def halo(centre, left, right, packed_left, packed_right, send, recv, chunk=None, skip=0):
+    def halo(centre, left, right, packed_left, packed_right, send, recv, chunk=None, takes=lambda dx, dy: True):
         copies = []
-        for number, (dx, dy) in enumerate(AROUND[skip:]):
+        for number, (dx, dy) in enumerate(AROUND):
+            if not takes(dx, dy):
+                continue
             if dy == 0:
                 if chunk is None:
                     src, dst = centre.at[:, from_rows[dx], :], centre.at[:, to_rows[dx], :]
@@ -113,8 +115,14 @@
     batch = members // CHUNKS
 
     def send_chunk(number):
-        return halo(ac, hl, hr, kl, kr, a_send.at[number], a_recv.at[number], pl.ds(number * batch, batch))
+        return halo(
+            ac, hl, hr, kl, kr, a_send.at[number], a_recv.at[number], pl.ds(number * batch, batch),
+            lambda dx, dy: dx != 0,
+        )
     a_copies = [send_chunk(0)]
+    a_lat = halo(
+        ac, hl, hr, kl, kr, a_send.at[0], a_recv.at[0], pl.ds(0, members), lambda dx, dy: dx == 0
+    )
     index = idx_ref[...]
     weight = wt_ref[...]
     at_row, at_col = index // cols, lax.rem(index, cols)
@@ -167,7 +175,10 @@
             )
             one.start()
             group.append(one)
-    f0_copies = s_copies + halo(f0c, f0l, f0r, k0l, k0r, f0_send, f0_recv, skip=2)
+    f0_lat = halo(f0c, f0l, f0r, k0l, k0r, f0_send, f0_recv, takes=lambda dx, dy: dx == 0)
+    f0_copies = s_copies + halo(
+        f0c, f0l, f0r, k0l, k0r, f0_send, f0_recv, takes=lambda dx, dy: dx != 0 and dy != 0
+    )
     a_copies.append(send_chunk(1))
     r, c = iota((cols, cols), 0), iota((cols, cols), 1)
     inside_low = jnp.where(lat > 0, 1.0, 0.0).astype(F32)
@@ -220,28 +231,12 @@
 
     lax.fori_loop(0, levels, level_matrices, 0)
     a_copies.append(send_chunk(2))
-    for number, (one, rim) in enumerate(zip(z_copies, (low, high))):
-        one.wait_recv()
-        passed = copy(
-            f0c.at[ours, rim, :], f0c.at[ours, rim, :],
-            z_send.at[4 + number], z_recv.at[4 + number], at(0, 0, twin),
-        )
-        passed.start()
-        f0_copies.append(passed)
-    for one in f0_copies:
-        one.wait_recv()
-    a_copies.append(send_chunk(3))
-    realign = jnp.where((r - spare == c - HALO * mem) & (r >= spare) & (r < spare + HALO), 1.0, 0.0)
-    sl[0] = dot(f0l[0], realign, HI)
-    sl[1] = dot(f0r[0], realign, HI)
-
     def lon_pass(l, u_hi, u_lo, which, matrix=nlon):
         depth = u_hi.shape[0]
         both = matrix[which, l] if matrix.shape[3] == depth else matrix[which, l, :, 0:depth]
         tall = dot(both, u_hi)
         return tall[0:rows] + tall[rows:] + dot(both[0:rows], u_lo)
 
-    every_row = (0, ext, 0)
     own_rows, rim_rows = (0, rows, 0), (rows, 2 * HALO, members * rows)
 
     def apply_members(centre, left, right, start, count, part, fresh):
@@ -287,13 +282,10 @@
     def parts(turn, which):
         for l in which:
             for k in range(members):
-                if turn == 0:
-                    u = ub[l, pl.ds(k * ext, ext), cols:2 * cols]
-                else:
-                    u = jnp.concatenate(
-                        [ub[l, pl.ds(base + k * size, size), cols:2 * cols] for _, size, base in (own_rows, rim_rows)],
-                        axis=0,
-                    )
+                u = jnp.concatenate(
+                    [ub[l, pl.ds(base + k * size, size), cols:2 * cols] for _, size, base in (own_rows, rim_rows)],
+                    axis=0,
+                )
                 hi, lo = split(u)
                 p_ref[turn, k, l] = math.sqrt(ce2) * lon_pass(l, hi, lo, 1)
 
@@ -325,10 +317,28 @@
             total = total + slots[o]
         return total
 
+    for one in a_lat + f0_lat:
+        one.wait_recv()
+    apply_members(f0c, f0l, f0r, 0, members, own_rows, True)
+    for number, (one, rim) in enumerate(zip(z_copies, (low, high))):
+        one.wait_recv()
+        passed = copy(
+            f0c.at[ours, rim, :], f0c.at[ours, rim, :],
+            z_send.at[4 + number], z_recv.at[4 + number], at(0, 0, twin),
+        )
+        passed.start()
+        f0_copies.append(passed)
+    a_copies.append(send_chunk(3))
+    for one in f0_copies:
+        one.wait_recv()
+    realign = jnp.where((r - spare == c - HALO * mem) & (r >= spare) & (r < spare + HALO), 1.0, 0.0)
+    sl[0] = dot(f0l[0], realign, HI)
+    sl[1] = dot(f0r[0], realign, HI)
+
     for number in range(CHUNKS):
         for one in a_copies[number]:
             one.wait_recv()
-        apply_members(f0c, f0l, f0r, number * batch, batch, every_row, number == 0)
+        apply_members(f0c, f0l, f0r, number * batch, batch, rim_rows, False)
     r0_copies = scatter_sum(yr.at[0], r0_send, r0_recv)
     apply_static(f0c, f0l, f0r)
     parts(0, (0, 1))
@@ -348,9 +358,8 @@
     for one in g_copies:
         one.wait_recv()
     pack(f1c, k1l, k1r)
-    f1_copies = halo(f1c, f1l, f1r, k1l, k1r, f1_send, f1_recv, skip=2)
-    f1_lat = [one for one, (dx, dy) in zip(f1_copies, AROUND[2:]) if dx == 0]
-    f1_corners = [one for one, (dx, dy) in zip(f1_copies, AROUND[2:]) if dx != 0]
+    f1_lat = halo(f1c, f1l, f1r, k1l, k1r, f1_send, f1_recv, takes=lambda dx, dy: dx == 0)
+    f1_corners = halo(f1c, f1l, f1r, k1l, k1r, f1_send, f1_recv, takes=lambda dx, dy: dx != 0 and dy != 0)
     for number, dx in enumerate((1, -1)):
         for o in range(n_mem):
             one = copy(
@@ -402,6 +411,10 @@
     sums = total_finish(gather_plane, plane_copies)
     line_copies = total_start(sums, gather_lon, lon // 2, line, so_send, so_recv)
     q1_copies = static_part(1, q1_send, q1_recv)
+    for one in q0_copies + q1_copies:
+        one.wait()
+    outs.append(pltpu.make_async_copy(ps_ref, static_out, out_sem.at[3]))
+    outs[-1].start()
     sums = total_finish(gather_lon, line_copies)
     row = sums[0:1]
 
@@ -417,16 +430,12 @@
     lam_ref[...] = jnp.where(lane == 0, alpha + alpha_next * g, alpha_next * h)
     outs.append(pltpu.make_async_copy(lam_ref, lam_out, out_sem.at[2]))
     outs[-1].start()
-    for one in q0_copies + q1_copies:
-        one.wait()
-    outs.append(pltpu.make_async_copy(ps_ref, static_out, out_sem.at[3]))
-    outs[-1].start()
     for one in outs:
         one.wait()
     for copies in a_copies:
         for one in copies:
             one.wait_send()
-    for one in z_copies + f0_copies + g_copies + c1_copies + f1_copies + plane_copies + line_copies:
+    for one in z_copies + f0_lat + f0_copies + g_copies + c1_copies + f1_lat + f1_corners + a_lat + plane_copies + line_copies:
         one.wait_send()
 
 

time: 63.3 us -> 62.6 us (0.989)
  no operation moved by 1% of the time
where the time goes in v4:
time: 62.6 us; the launch traced here: 62.5 us
  Pallas kernels  61.9 us (99%)
  between operations  0.64 us (1%)
    pallas_call x1, Pallas kernels, per_device(): pl.pallas_call(lambda *refs: kernel(dims, *refs), out_shape=(jax.ShapeDty...  59.3 us
    pallas_call x1, Pallas kernels, per_device(): pl.pallas_call(combine, out_shape=(jax.ShapeDtypeStruct((members, levels,...  2.53 us

profile of v4, /device:TPU:1, one launch (start us, length us, event | category | flops | bytes accessed | tf_op | source)
XLA Modules:
  0.0 62.5 jit_solution(3339643102614406168)
XLA Ops:
  0.6 59.3 %shard_map.77 = (f32[2,8,4,64,128]{4,3,2,1,0:T(8,128)}, f32[2,4,64,128]{3,2,1,0:T(8,128)}, f32[8,128]{1,0:T(8,128)}) custom-call(s32[2,4]{1,0:T(2,128)} %refs_0_.1, bf16[8,4,64,128]{3,2,1,0:T(8,128)(2,1)} %refs_1_.1, f32[4,64,128]{2,1,0:T(8,128)} %refs_2_.1, s32[1,2048]{1,0:T(1,128)} %bitcast.3, f32[1,2048]{1,0:T(1,128)} %bitcast.4, f32[1,2048]{1,0:T(1,128)} %bitcast.5), custom_call_target="tpu_custom_call" | custom-call | tf_op jit(solution)/shard_map/pallas_call | solution.py:474
  60.0 2.5 %shard_map.78 = (f32[8,4,64,128]{3,2,1,0:T(8,128)}, f32[4,64,128]{2,1,0:T(8,128)}) custom-call(f32[2,8,4,64,128]{4,3,2,1,0:T(8,128)} %get-tuple-element.5.ens_in, f32[2,4,64,128]{3,2,1,0:T(8,128)} %get-tuple-element.6.static_in, f32[8,128]{1,0:T(8,128)} %get-tuple-element.7.lam_in), custom_call_target="tpu_custom_call" | custom-call | tf_op jit(solution)/shard_map/pallas_call | solution.py:530

commit v5 on v4

--- a/solution.py
+++ b/solution.py
@@ -57,7 +57,7 @@
     across = 1 - 2 * parity
     plane = [(tx * across, ol, om) for tx in range(2) for ol in range(n_lat) for om in range(n_mem)][1:]
     line = [(o, 0, 0) for o in range(2, n_lon, 2)]
-    partners = plane + line + [(-across, dy, 0) for dy in (0, 1, -1)] + [(-across, 0, o) for o in range(1, n_mem)]
+    partners = line + plane[::-1] + [(-across, dy, 0) for dy in (0, 1, -1)] + [(-across, 0, o) for o in range(1, n_mem)]
     barrier = pltpu.get_barrier_semaphore()
     for partner in partners:
         pl.semaphore_signal(barrier, inc=1, device_id=at(*partner), device_id_type=MESH)

time: 62.6 us -> 62.6 us (level)
  no operation moved by 1% of the time
where the time goes in v5:
time: 62.6 us; the launch traced here: 62.5 us
  Pallas kernels  61.8 us (99%)
  between operations  0.64 us (1%)
    pallas_call x1, Pallas kernels, per_device(): pl.pallas_call(lambda *refs: kernel(dims, *refs), out_shape=(jax.ShapeDty...  59.3 us
    pallas_call x1, Pallas kernels, per_device(): pl.pallas_call(combine, out_shape=(jax.ShapeDtypeStruct((members, levels,...  2.53 us

profile of v5, /device:TPU:1, one launch (start us, length us, event | category | flops | bytes accessed | tf_op | source)
XLA Modules:
  0.0 62.5 jit_solution(2353214708386428202)
XLA Ops:
  0.6 59.3 %shard_map.77 = (f32[2,8,4,64,128]{4,3,2,1,0:T(8,128)}, f32[2,4,64,128]{3,2,1,0:T(8,128)}, f32[8,128]{1,0:T(8,128)}) custom-call(s32[2,4]{1,0:T(2,128)} %refs_0_.1, bf16[8,4,64,128]{3,2,1,0:T(8,128)(2,1)} %refs_1_.1, f32[4,64,128]{2,1,0:T(8,128)} %refs_2_.1, s32[1,2048]{1,0:T(1,128)} %bitcast.3, f32[1,2048]{1,0:T(1,128)} %bitcast.4, f32[1,2048]{1,0:T(1,128)} %bitcast.5), custom_call_target="tpu_custom_call" | custom-call | tf_op jit(solution)/shard_map/pallas_call | solution.py:474
  59.9 2.5 %shard_map.78 = (f32[8,4,64,128]{3,2,1,0:T(8,128)}, f32[4,64,128]{2,1,0:T(8,128)}) custom-call(f32[2,8,4,64,128]{4,3,2,1,0:T(8,128)} %get-tuple-element.5.ens_in, f32[2,4,64,128]{3,2,1,0:T(8,128)} %get-tuple-element.6.static_in, f32[8,128]{1,0:T(8,128)} %get-tuple-element.7.lam_in), custom_call_target="tpu_custom_call" | custom-call | tf_op jit(solution)/shard_map/pallas_call | solution.py:530
